TPU v7x, 32 devices: a whole 2x2x4 slice. The times are simulated.
32 devices in a mesh: win: 8 (over z, x), band: 4 (over y, core).
Axes of the slice: x: 2, y: 2, z: 4, core: 2. Of those that a mesh axis runs over, the one named last changes fastest.
Arguments:
- vis: bfloat16 [32768, 2, 1024], P(('win', 'band')), may hold values from -6 to 6
- inv_noise: float32 [32768, 1024], P(('win', 'band')), may hold values from 0.14 to 4.2
- assign: int32 [32768], P(('win', 'band')), may hold values from 0 to 63, as said below
- taper_bank: float32 [4, 1024], replicated, may hold values from 0.2 to 1.25
- taper_pick: int32 [32], replicated, may hold values from 0 to 3
Outputs:
- window_fn: float32 [32, 512, 512], P(('win', 'band'))
Inputs may be any that keep to these rules, and one draw needn't show every extreme that they name: `assign`: in the rows of one device no value is named by more than 32 pairs; one value is named by exactly 32 pairs in the rows of every device.
All inputs are finite; a program needn't handle non-finite values.
Results may differ from a plain program's by a relative error of at most 0.0014.
Values may be sent and summed in bfloat16 or wider, within the bound.
No kernel may reach another device: no remote copies, remote signals or barrier semaphores. Data moves between devices by JAX's collectives and lax.ppermute only.
A program may use at most 64 MiB of HBM per device.

v0:
```python
import jax
import jax.numpy as jnp
from jax import lax
from jax.sharding import PartitionSpec as P

FREQ = 1024
P_SIZE = 512
TAPERS = 4


ridge_share = 0.1


def delay_table():
    delays = jnp.arange(P_SIZE, dtype=jnp.int32)
    channel = jnp.arange(FREQ, dtype=jnp.int32)
    phases = (delays[:, None] * channel[None, :] % FREQ).astype(jnp.float32) * (2.0 * jnp.pi / FREQ)
    cosine_rows = jnp.cos(phases).astype(jnp.bfloat16).T
    sine_rows = jnp.sin(phases).astype(jnp.bfloat16).T
    top_block = jnp.concatenate([cosine_rows, -sine_rows], axis=1)
    low_block = jnp.concatenate([sine_rows, cosine_rows], axis=1)
    return jnp.concatenate([top_block, low_block], axis=0)


def local(vis, inv_noise, assign, taper_bank, taper_pick):
    win_size = lax.axis_size("win")
    band_size = lax.axis_size("band")
    windows = win_size * band_size
    pair_count = assign.shape[0]
    capacity = pair_count // windows
    spectral = 2 * P_SIZE
    group_lanes = 2 * windows
    window_ids = assign // 2
    window_match = (window_ids[:, None] == jnp.arange(windows, dtype=jnp.int32)[None, :]).astype(
        jnp.int32
    )
    picked_taper = jnp.sum(window_match * taper_pick[None, :], axis=1)
    taper_match = (picked_taper[:, None] == jnp.arange(TAPERS, dtype=jnp.int32)[None, :]).astype(
        jnp.float32
    )
    taper_rows = jnp.dot(
        taper_match, taper_bank, precision=lax.Precision.HIGHEST, preferred_element_type=jnp.float32
    )
    weighted = (taper_rows[:, None, :] * inv_noise[:, None, :] * vis.astype(jnp.float32)).astype(
        jnp.bfloat16
    )
    spectra = jnp.dot(
        weighted.reshape(pair_count, 2 * FREQ), delay_table(), preferred_element_type=jnp.float32
    ).astype(jnp.bfloat16)
    ident_match = (assign[:, None] == jnp.arange(group_lanes, dtype=jnp.int32)[None, :]).astype(
        jnp.bfloat16
    )
    position = jnp.arange(pair_count, dtype=jnp.int32)
    before = (position[None, :] < position[:, None]).astype(jnp.bfloat16)
    earlier = jnp.dot(before, ident_match, preferred_element_type=jnp.float32)
    slot_rank = jnp.sum(earlier * ident_match.astype(jnp.float32), axis=1).astype(jnp.int32)
    slot_index = assign * capacity + slot_rank
    source_row = (
        jnp.full((group_lanes * capacity,), pair_count, jnp.int32).at[slot_index].set(position)
    )
    padded = jnp.concatenate([spectra, jnp.zeros((1, spectral), jnp.bfloat16)], axis=0)
    outgoing = jnp.take(padded, source_row, axis=0)
    incoming = lax.all_to_all(outgoing, ("win", "band"), split_axis=0, concat_axis=0, tiled=True)
    incoming = incoming.reshape(windows, 2, capacity, spectral)
    moments = jnp.einsum("sgcm,sgcn->gmn", incoming, incoming, preferred_element_type=jnp.float32)
    real_part = moments[:, :P_SIZE, :P_SIZE] + moments[:, P_SIZE:, P_SIZE:]
    imag_part = moments[:, P_SIZE:, :P_SIZE] - moments[:, :P_SIZE, P_SIZE:]
    fisher = 0.5 * (real_part[0] * real_part[1] + imag_part[0] * imag_part[1])
    local_trace = jnp.trace(fisher)
    diag_total = lax.psum(local_trace, ("win", "band"))
    ridge_term = ridge_share * diag_total / (windows * P_SIZE)
    factor = jnp.linalg.cholesky(fisher + ridge_term * jnp.eye(P_SIZE, dtype=jnp.float32))
    window = factor.T
    row_sums = jnp.sum(window, axis=1)
    divisor = jnp.maximum(row_sums, jnp.diagonal(window))
    return (window / divisor[:, None])[None]


def solution(mesh):
    in_specs = (
        P(("win", "band"), None, None),
        P(("win", "band"), None),
        P(("win", "band")),
        P(),
        P(),
    )
    out_specs = P(("win", "band"), None, None)
    return jax.shard_map(local, mesh=mesh, in_specs=in_specs, out_specs=out_specs, check_vma=False)
```

profile of v0, /device:TPU:0, one launch (start us, length us, event | category | flops | bytes accessed | tf_op | source)
XLA Modules:
  0.0 313.7 jit_solution(5680042232156758961)
XLA Ops:
  0.0 8.5 %sine_convert_fusion = (bf16[1024,512]{1,0:T(8,128)(2,1)S(1)}, bf16[1024,512]{1,0:T(8,128)(2,1)S(1)}) fusion(), kind=kLoop, calls=%fused_computation.25 | loop fusion | flops 8388608 | bytes 2097152 | tf_op jit(solution)/shard_map/convert_element_type | solution.py:19
  8.5 8.0 %fusion.26 = bf16[1024,512]{1,0:T(8,128)(2,1)S(1)} fusion(), kind=kLoop, calls=%fused_computation.54 | loop fusion | flops 9437184 | bytes 1048576 | tf_op jit(solution)/shard_map/neg | solution.py:20
  17.1 4.3 %scatter_custom_fusion = s32[2048]{0:T(1024)S(1)} fusion(s32[1024]{0:T(1024)S(1)} %get-tuple-element.17, s32[1024]{0:T(1024)S(1)} %iota.124, s32[]{:T(128)} %constant.188.clone.1), kind=kCustom, calls=%fused_computation.91 | custom fusion | bytes 8196 | tf_op jit(solution)/shard_map/scatter | solution.py:59
  21.6 4.3 %convolution_multiply_fusion = f32[1024,1024]{1,0:T(8,128)S(1)} fusion(f32[1024,1024]{1,0:T(8,128)} %param.6, f32[4,1024]{1,0:T(4,128)S(1)} %copy-done, s32[1024]{0:T(1024)S(1)} %select_reduce_fusion.1), kind=kOutput, calls=%fused_computation.19 | convolution fusion | flops 51384320 | bytes 8409088 | tf_op jit(solution)/shard_map/dot_general | solution.py:41
  25.9 4.9 %multiply_convert_fusion = bf16[1024,2,1024]{2,1,0:T(2,128)(2,1)S(1)} fusion(bf16[1024,2,1024]{2,1,0:T(2,128)(2,1)S(1)} %copy-done.1, f32[1024,1024]{1,0:T(8,128)S(1)} %convolution_multiply_fusion), kind=kLoop, calls=%fused_computation.3 | loop fusion | flops 6291456 | bytes 12582912 | tf_op jit(solution)/shard_map/convert_element_type | solution.py:44
  30.8 3.3 %copy.66 = bf16[128,8,2,1024]{3,1,2,0:T(8,128)(2,1)} copy(bf16[128,8,2,1024]{3,2,1,0:T(2,128)(2,1)S(1)} %bitcast.43) | data formatting | bytes 8388608
  34.3 20.6 %fusion.15 = bf16[1024,1024]{1,0:T(8,128)(2,1)S(1)} fusion(bf16[1024,2048]{1,0:T(8,128)(2,1)} %bitcast.45, bf16[1024,512]{1,0:T(8,128)(2,1)S(1)} %get-tuple-element.20, bf16[1024,512]{1,0:T(8,128)(2,1)S(1)} %get-tuple-element.19, bf16[1024,512]{1,0:T(8,128)(2,1)S(1)} %fusion.26), kind=kOutput, calls=%fused_computation.30 | convolution fusion | flops 4312793088 | bytes 9437184 | tf_op jit(solution)/shard_map/dot_general | solution.py:47
  55.0 9.8 %gather_fusion = bf16[2048,1024]{1,0:T(8,128)(2,1)} fusion(bf16[1025,1024]{1,0:T(8,128)(2,1)S(1)} %concatenate.19, s32[2048]{0:T(1024)S(1)} %fusion.41), kind=kCustom, calls=%fused_computation | custom fusion | bytes 8396800 | tf_op jit(solution)/shard_map/jit(_take)/gather | solution.py:62
  64.9 3.8 %broadcast_select_fusion = bf16[32,64,1024]{2,1,0:T(8,128)(2,1)} fusion(bf16[32,64,1024]{2,1,0:T(8,128)(2,1)} %bitcast.44, pred[32,64]{1,0:T(8,128)(4,1)S(1)} %broadcast_in_dim.50), kind=kLoop, calls=%fused_computation.13 | loop fusion | flops 2097152 | bytes 8390656 | tf_op jit(solution)/shard_map/jit(_take)/select_n | solution.py:62
  68.7 7.5 %all-to-all-start = ((bf16[32,64,1024]{2,1,0:T(8,128)(2,1)}), bf16[32,64,1024]{2,1,0:T(8,128)(2,1)}, u32[]{:S(2)}, u32[]{:S(2)}) async-start(bf16[32,64,1024]{2,1,0:T(8,128)(2,1)} %broadcast_select_fusion), calls=%async_computation | async-start | bytes 8388608 | tf_op jit(solution)/shard_map/all_to_all | solution.py:63
  76.1 94.2 %all-to-all-done = bf16[32,64,1024]{2,1,0:T(8,128)(2,1)} async-done(((bf16[32,64,1024]{2,1,0:T(8,128)(2,1)}), bf16[32,64,1024]{2,1,0:T(8,128)(2,1)}, u32[]{:S(2)}, u32[]{:S(2)}) %all-to-all-start) | async-done | bytes 4194336 | tf_op jit(solution)/shard_map/all_to_all | solution.py:63
  170.4 4.5 %copy.46 = bf16[32,64,1024]{2,0,1:T(8,128)(2,1)S(1)} copy(bf16[32,64,1024]{2,1,0:T(8,128)(2,1)} %all-to-all-done) | data formatting | bytes 8388608 | tf_op jit(solution)/shard_map/all_to_all | solution.py:63
  174.9 4.7 %convolution_bitcast_fusion = f32[2,1024,1024]{1,2,0:T(8,128)S(1)} fusion(bf16[32,2,32,1024]{3,0,2,1:T(8,128)(2,1)S(1)} %bitcast.46), kind=kOutput, calls=%fused_computation.15 | convolution fusion | flops 4294967296 | bytes 12582912 | tf_op jit(solution)/shard_map/sgcm,sgcn->gmn/dot_general | solution.py:65
  180.6 1.1 select_reduce_fusion
  181.7 39.5 %psum.7 = f32[]{:T(128)} all-reduce(f32[]{:T(128)} %get-tuple-element.5), channel_id=1, replica_groups=mesh['win'=8,'band'=4] {'win','band'}, use_global_device_ids=true, to_apply=%region_4.5 | all-reduce | flops 1 | bytes 8 | tf_op jit(solution)/shard_map/psum | solution.py:70
  222.5 11.7 %cholesky.103 = f32[128,128]{1,0:T(8,128)S(1)} custom-call(f32[128,128]{1,0:T(8,128)S(1)} %cholesky.263), custom_call_target="Cholesky" | custom-call | tf_op jit(solution)/shard_map/jit(cholesky)/cholesky | solution.py:72
  234.3 9.8 %custom-call.27 = f32[1,128,128]{1,2,0:T(8,128)S(1)} custom-call(f32[1,128,128]{2,1,0:T(8,128)S(1)} %get-tuple-element.16), custom_call_target="InvertDiagBlocksLowerTriangular" | custom-call | tf_op jit(solution)/shard_map/jit(cholesky)/cholesky | solution.py:72
  244.8 11.7 %cholesky.215 = f32[128,128]{1,0:T(8,128)S(1)} custom-call(f32[128,128]{1,0:T(8,128)S(1)} %cholesky.267), custom_call_target="Cholesky" | custom-call | tf_op jit(solution)/shard_map/jit(cholesky)/cholesky | solution.py:72
  256.9 10.0 %custom-call.28 = f32[1,128,128]{1,2,0:T(8,128)S(1)} custom-call(f32[1,128,128]{2,1,0:T(8,128)S(1)} %get-tuple-element.14), custom_call_target="InvertDiagBlocksLowerTriangular" | custom-call | tf_op jit(solution)/shard_map/jit(cholesky)/cholesky | solution.py:72
  268.0 11.7 %cholesky.236 = f32[128,128]{1,0:T(8,128)S(1)} custom-call(f32[128,128]{1,0:T(8,128)S(1)} %cholesky.272), custom_call_target="Cholesky" | custom-call | tf_op jit(solution)/shard_map/jit(cholesky)/cholesky | solution.py:72
  279.8 9.8 %custom-call.29 = f32[1,128,128]{1,2,0:T(8,128)S(1)} custom-call(f32[1,128,128]{2,1,0:T(8,128)S(1)} %get-tuple-element.12), custom_call_target="InvertDiagBlocksLowerTriangular" | custom-call | tf_op jit(solution)/shard_map/jit(cholesky)/cholesky | solution.py:72
  290.4 11.7 %cholesky.253 = f32[128,128]{1,0:T(8,128)S(1)} custom-call(f32[128,128]{1,0:T(8,128)S(1)} %convolution_subtract_fusion.2), custom_call_target="Cholesky" | custom-call | tf_op jit(solution)/shard_map/jit(cholesky)/cholesky | solution.py:72
  307.6 4.5 %gather_fusion.1 = f32[512]{0:T(512)S(1)} fusion(f32[512,512]{1,0:T(8,128)S(1)} %get-tuple-element.10, s32[512]{0:T(512)S(1)} %bitcast.42), kind=kCustom, calls=%fused_computation.1 | custom fusion | bytes 8192 | tf_op jit(solution)/shard_map/jit(diagonal)/cond/branch_0_fun/gather | solution.py:75
  312.2 1.1 divide_bitcast_fusion
  (50 shorter events, 8.6 us)
Async XLA Ops:
  0.0 21.6 %copy-start = (f32[4,1024]{1,0:T(4,128)S(1)}, f32[4,1024]{1,0:T(4,128)}, u32[]{:S(2)}) copy-start(f32[4,1024]{1,0:T(4,128)} %param.8) | copy-start | bytes 49156
  0.0 16.5 %copy-start.2 = (s32[1024]{0:T(1024)S(1)}, s32[1024]{0:T(1024)}, u32[]{:S(2)}) copy-start(s32[1024]{0:T(1024)} %param.7) | copy-start | bytes 12292
  0.0 21.5 %copy-start.3 = (s32[32]{0:T(128)S(1)}, s32[32]{0:T(128)}, u32[]{:S(2)}) copy-start(s32[32]{0:T(128)} %param.9) | copy-start | bytes 388
  21.6 4.3 %copy-start.1 = (bf16[1024,2,1024]{2,1,0:T(2,128)(2,1)S(1)}, bf16[1024,2,1024]{2,1,0:T(2,128)(2,1)}, u32[]{:S(2)}) copy-start(bf16[1024,2,1024]{2,1,0:T(2,128)(2,1)} %param.5) | copy-start | bytes 12582916
  68.7 101.7 %all-to-all-start = ((bf16[32,64,1024]{2,1,0:T(8,128)(2,1)}), bf16[32,64,1024]{2,1,0:T(8,128)(2,1)}, u32[]{:S(2)}, u32[]{:S(2)}) async-start(bf16[32,64,1024]{2,1,0:T(8,128)(2,1)} %broadcast_select_fusion), calls=%async_computation | async-start | bytes 8388608 | tf_op jit(solution)/shard_map/all_to_all | solution.py:63
where the time goes:
time: 318 us; the launch traced here: 314 us
  other arithmetic  108 us (34%)
  waiting for transfers between devices  94.2 us (30%)
  blocking collectives  39.5 us (12%)
  matrix products  32.5 us (10%)
  local copies, waits for them, and re-layouts  27.8 us (9%)
  starting transfers between devices  7.46 us (2%)
  between operations  4 us (1%)
    all_to_all x1, waiting for transfers between devices, local(): lax.all_to_all(outgoing, ('win', 'band'), split_axis=0, concat_axis=0, ti...  94.2 us
    another operation x15, other arithmetic, local(): jnp.linalg.cholesky(fisher + ridge_term * jnp.eye(P_SIZE, dtype=jnp.float...  79.3 us
    psum x1, blocking collectives, local(): diag_total = lax.psum(local_trace, ('win', 'band'))  39.5 us
    dot_general x1, matrix products, local(): jnp.dot(weighted.reshape(pair_count, 2 * FREQ), delay_table(), preferred_...  20.6 us
    gather x1, local copies, waits for them, and re-layouts, local(): outgoing = jnp.take(padded, source_row, axis=0)  9.83 us
    convert_element_type x1, other arithmetic, delay_table(): sine_rows = jnp.sin(phases).astype(jnp.bfloat16).T  8.47 us
    neg x1, other arithmetic, delay_table(): top_block = jnp.concatenate([cosine_rows, -sine_rows], axis=1)  7.98 us
    all_to_all x1, starting transfers between devices, local(): lax.all_to_all(outgoing, ('win', 'band'), split_axis=0, concat_axis=0, ti...  7.46 us
  transfers between devices with their start and end apart: 1, of which 1 were waited for; matrix products, arithmetic and copies ran while one was open for 0% of the time, Pallas kernels for 0%

commit v1 on v0

--- a/solution.py
+++ b/solution.py
@@ -1,6 +1,8 @@
 import jax
 import jax.numpy as jnp
 from jax import lax
+from jax.experimental import pallas as pl
+from jax.experimental.pallas import tpu as pltpu
 from jax.sharding import PartitionSpec as P
 
 FREQ = 1024
@@ -20,6 +22,103 @@
     top_block = jnp.concatenate([cosine_rows, -sine_rows], axis=1)
     low_block = jnp.concatenate([sine_rows, cosine_rows], axis=1)
     return jnp.concatenate([top_block, low_block], axis=0)
+
+
+STEP = 16
+LANE = 128
+
+
+def split_halves(x):
+    high = x.astype(jnp.bfloat16)
+    low = (x - high.astype(jnp.float32)).astype(jnp.bfloat16)
+    return high, low
+
+
+def cross(left, right):
+    return lax.dot_general(left, right, (((0,), (0,)), ((), ())), preferred_element_type=jnp.float32)
+
+
+def factor_kernel(ridge_ref, fisher_ref, out_ref, work_ref, left_ref, right_ref):
+    size = fisher_ref.shape[0]
+    ridge = ridge_ref[0:1, 0:1]
+    rows = lax.broadcasted_iota(jnp.int32, (STEP, LANE), 0)
+    lanes = lax.broadcasted_iota(jnp.int32, (STEP, LANE), 1)
+    square_r = lax.broadcasted_iota(jnp.int32, (LANE, LANE), 0)
+    square_c = lax.broadcasted_iota(jnp.int32, (LANE, LANE), 1)
+    eye = jnp.where(square_r == square_c, jnp.broadcast_to(ridge, (LANE, LANE)), 0.0)
+    for p in range(size // LANE):
+        base = p * LANE
+        tail = slice(base, base + LANE)
+        work_ref[tail, base:] = fisher_ref[tail, base:]
+        work_ref[tail, tail] = fisher_ref[tail, tail] + eye
+    for p in range(size // LANE):
+        base = p * LANE
+        tiles = (size - base) // LANE
+        for b in range(LANE // STEP):
+            k = base + STEP * b
+            panel = [work_ref[k : k + STEP, base + LANE * t : base + LANE * (t + 1)] for t in range(tiles)]
+            columns = [
+                jnp.broadcast_to(panel[0][:, STEP * b + c : STEP * b + c + 1], (STEP, LANE)) for c in range(STEP)
+            ]
+            scale = jnp.zeros((STEP, LANE), jnp.float32)
+            for j in range(STEP):
+                pivot = jnp.broadcast_to(columns[j][j : j + 1, :], (STEP, LANE))
+                root = lax.rsqrt(pivot)
+                scale = jnp.where(rows == j, root, scale)
+                if j < STEP - 1:
+                    ratio = jnp.where(rows > j, columns[j] * (root * root), 0.0)
+                    for c in range(j + 1, STEP):
+                        columns[c] = columns[c] - ratio * jnp.broadcast_to(columns[c][j : j + 1, :], (STEP, LANE))
+                    panel = [x - ratio * jnp.broadcast_to(x[j : j + 1, :], (STEP, LANE)) for x in panel]
+            panel = [x * scale for x in panel]
+            panel[0] = jnp.where(lanes >= rows + STEP * b, panel[0], 0.0)
+            halves = [split_halves(x) for x in panel]
+            span = slice(STEP * b, STEP * (b + 1))
+            if b < LANE // STEP - 1:
+                left = jnp.concatenate([halves[0][0], halves[0][0], halves[0][1]], axis=0)
+                for t in range(tiles):
+                    right = jnp.concatenate([halves[t][0], halves[t][1], halves[t][0]], axis=0)
+                    update = cross(left, right)
+                    below = slice(k + STEP, base + LANE)
+                    across = slice(base + LANE * t, base + LANE * (t + 1))
+                    work_ref[below, across] = work_ref[below, across] - update[STEP * (b + 1) :, :]
+            for t in range(1, tiles):
+                across = slice(base + LANE * t, base + LANE * (t + 1))
+                left_ref[span, across] = halves[t][0]
+                right_ref[span, across] = halves[t][1]
+            total = panel[0]
+            for x in panel[1:]:
+                total = total + x
+            sums = jnp.sum(total, axis=1, keepdims=True)
+            peak = jnp.sum(jnp.where(lanes == rows + STEP * b, panel[0], 0.0), axis=1, keepdims=True)
+            inverse = jnp.broadcast_to(1.0 / jnp.maximum(sums, peak), (STEP, LANE))
+            for t in range(p):
+                out_ref[k : k + STEP, LANE * t : LANE * (t + 1)] = jnp.zeros((STEP, LANE), jnp.float32)
+            for t in range(tiles):
+                out_ref[k : k + STEP, base + LANE * t : base + LANE * (t + 1)] = panel[t] * inverse
+        for q in range(p + 1, size // LANE):
+            mine = slice(LANE * q, LANE * (q + 1))
+            rest = slice(LANE * q, size)
+            high, low = left_ref[:, mine], right_ref[:, mine]
+            left = jnp.concatenate([high, high, low], axis=0)
+            right = jnp.concatenate([left_ref[:, rest], right_ref[:, rest], left_ref[:, rest]], axis=0)
+            work_ref[mine, rest] = work_ref[mine, rest] - cross(left, right)
+
+
+def factor_rows(fisher, ridge):
+    size = fisher.shape[0]
+    return pl.pallas_call(
+        factor_kernel,
+        out_shape=jax.ShapeDtypeStruct((size, size), jnp.float32),
+        in_specs=[pl.BlockSpec(memory_space=pltpu.VMEM)] * 2,
+        out_specs=pl.BlockSpec(memory_space=pltpu.VMEM),
+        scratch_shapes=[
+            pltpu.VMEM((size, size), jnp.float32),
+            pltpu.VMEM((LANE, size), jnp.bfloat16),
+            pltpu.VMEM((LANE, size), jnp.bfloat16),
+        ],
+        name="factor_rows",
+    )(jnp.broadcast_to(ridge, (8, LANE)), fisher)
 
 
 def local(vis, inv_noise, assign, taper_bank, taper_pick):
@@ -67,13 +166,10 @@
     imag_part = moments[:, P_SIZE:, :P_SIZE] - moments[:, :P_SIZE, P_SIZE:]
     fisher = 0.5 * (real_part[0] * real_part[1] + imag_part[0] * imag_part[1])
     local_trace = jnp.trace(fisher)
-    diag_total = lax.psum(local_trace, ("win", "band"))
+    shared = jnp.broadcast_to(local_trace, (windows,))
+    diag_total = jnp.sum(lax.all_to_all(shared, ("win", "band"), 0, 0, tiled=True))
     ridge_term = ridge_share * diag_total / (windows * P_SIZE)
-    factor = jnp.linalg.cholesky(fisher + ridge_term * jnp.eye(P_SIZE, dtype=jnp.float32))
-    window = factor.T
-    row_sums = jnp.sum(window, axis=1)
-    divisor = jnp.maximum(row_sums, jnp.diagonal(window))
-    return (window / divisor[:, None])[None]
+    return factor_rows(fisher, ridge_term)[None]
 
 
 def solution(mesh):

time: 318 us -> 206 us (0.65); the launches traced: 314 us -> 206 us
  waiting for transfers between devices: 94.2 us -> 0 us
  other arithmetic: 108 us -> 28 us
  blocking collectives: 39.5 us -> 111 us
  Pallas kernels: 0 us -> 17.6 us
  local copies, waits for them, and re-layouts: 27.8 us -> 19.3 us
  starting transfers between devices: 7.46 us -> 0 us
  matrix products: 32.5 us -> 29.1 us
  between operations: 4 us -> 0.81 us
    all_to_all x0 -> x2, blocking collectives: none -> 111 us  [the longest x1 101 us: local(): lax.all_to_all(outgoing, ('win', 'band'), split_axis=0, concat_axis=0, ti...]
    all_to_all x1 -> x0, waiting for transfers between devices: 94.2 us -> none  [local(): lax.all_to_all(outgoing, ('win', 'band'), split_axis=0, concat_axis=0, ti...]
    another operation x15 -> x0, other arithmetic: 79.3 us -> none  [local(): jnp.linalg.cholesky(fisher + ridge_term * jnp.eye(P_SIZE, dtype=jnp.float...]
    psum x1 -> x0, blocking collectives: 39.5 us -> none  [local(): diag_total = lax.psum(local_trace, ('win', 'band'))]
    pallas_call x0 -> x1, Pallas kernels: none -> 17.6 us  [factor_rows(): pl.pallas_call(factor_kernel, out_shape=jax.ShapeDtypeStruct((size, size)...]
    all_to_all x1 -> x0, starting transfers between devices: 7.46 us -> none  [local(): lax.all_to_all(outgoing, ('win', 'band'), split_axis=0, concat_axis=0, ti...]
    gather x1 -> x0, local copies, waits for them, and re-layouts: 4.52 us -> none  [local(): divisor = jnp.maximum(row_sums, jnp.diagonal(window))]
  transfers between devices with their start and end apart: 1 -> 0, of which waited for: 1 -> 0; matrix products, arithmetic and copies ran while one was open for 0% -> 0% of each run, Pallas kernels for 0% -> 0%
where the time goes in v1:
time: 206 us
  blocking collectives  111 us (54%)
  matrix products  29.1 us (14%)
  other arithmetic  28 us (14%)
  local copies, waits for them, and re-layouts  19.3 us (9%)
  Pallas kernels  17.6 us (9%)
    all_to_all x1, blocking collectives, local(): lax.all_to_all(outgoing, ('win', 'band'), split_axis=0, concat_axis=0, ti...  101 us
    dot_general x1, matrix products, local(): jnp.dot(weighted.reshape(pair_count, 2 * FREQ), delay_table(), preferred_...  18.9 us
    pallas_call x1, Pallas kernels, factor_rows(): pl.pallas_call(factor_kernel, out_shape=jax.ShapeDtypeStruct((size, size)...  17.6 us
    all_to_all x1, blocking collectives, local(): lax.all_to_all(shared, ('win', 'band'), 0, 0, tiled=True)  10.7 us
    gather x1, local copies, waits for them, and re-layouts, local(): outgoing = jnp.take(padded, source_row, axis=0)  9.67 us
    convert_element_type x1, other arithmetic, delay_table(): sine_rows = jnp.sin(phases).astype(jnp.bfloat16).T  8.48 us
    neg x1, other arithmetic, delay_table(): top_block = jnp.concatenate([cosine_rows, -sine_rows], axis=1)  7.98 us
    dot_general x1, matrix products, local(): jnp.einsum('sgcm,sgcn->gmn', incoming, incoming, preferred_element_type=j...  4.56 us

profile of v1, /device:TPU:0, one launch (start us, length us, event | category | flops | bytes accessed | tf_op | source)
XLA Modules:
  0.0 206.1 jit_solution(13269689876444563098)
XLA Ops:
  0.0 1.4 fusion.19
  1.4 0.7 compare_select_fusion.1
  2.1 4.3 %scatter_custom_fusion = s32[2048]{0:T(1024)S(1)} fusion(s32[1024]{0:T(1024)S(1)} %get-tuple-element.9, s32[1024]{0:T(1024)S(1)} %iota.45, s32[]{:T(128)} %constant.53.clone.1), kind=kCustom, calls=%fused_computation.57 | custom fusion | bytes 8196 | tf_op jit(solution)/shard_map/scatter | solution.py:158
  6.4 8.0 %fusion.23 = bf16[1024,512]{1,0:T(8,128)(2,1)S(1)} fusion(), kind=kLoop, calls=%fused_computation.40 | loop fusion | flops 9437184 | bytes 1048576 | tf_op jit(solution)/shard_map/neg | solution.py:22
  14.4 8.5 %sine_convert_fusion = (bf16[1024,512]{1,0:T(8,128)(2,1)S(1)}, bf16[1024,512]{1,0:T(8,128)(2,1)S(1)}) fusion(), kind=kLoop, calls=%fused_computation.24 | loop fusion | flops 8388608 | bytes 2097152 | tf_op jit(solution)/shard_map/convert_element_type | solution.py:21
  22.9 0.1 broadcast_in_dim.49
  23.0 0.1 select_reduce_fusion.1
  23.1 4.3 %convolution_multiply_fusion = f32[1024,1024]{1,0:T(8,128)S(1)} fusion(f32[1024,1024]{1,0:T(8,128)} %param.6, f32[4,1024]{1,0:T(4,128)S(1)} %copy-done, s32[1024]{0:T(1024)S(1)} %select_reduce_fusion.1), kind=kOutput, calls=%fused_computation.18 | convolution fusion | flops 51384320 | bytes 8409088 | tf_op jit(solution)/shard_map/dot_general | solution.py:140
  27.4 4.5 %multiply_convert_fusion = bf16[1024,2,1024]{2,1,0:T(2,128)(2,1)S(1)} fusion(bf16[1024,2,1024]{2,1,0:T(2,128)(2,1)S(1)} %copy-done.1, f32[1024,1024]{1,0:T(8,128)S(1)} %convolution_multiply_fusion), kind=kLoop, calls=%fused_computation.2 | loop fusion | flops 6291456 | bytes 12582912 | tf_op jit(solution)/shard_map/convert_element_type | solution.py:143
  31.9 1.4 copy.15
  33.3 18.9 %fusion.15 = bf16[1024,1024]{1,0:T(8,128)(2,1)S(1)} fusion(bf16[1024,2048]{1,0:T(8,128)(2,1)S(1)} %bitcast.18, bf16[1024,512]{1,0:T(8,128)(2,1)S(1)} %get-tuple-element.12, bf16[1024,512]{1,0:T(8,128)(2,1)S(1)} %get-tuple-element.11, bf16[1024,512]{1,0:T(8,128)(2,1)S(1)} %fusion.23), kind=kOutput, calls=%fused_computation.29 | convolution fusion | flops 4312793088 | bytes 9437184 | tf_op jit(solution)/shard_map/dot_general | solution.py:146
  52.2 0.2 concatenate.15
  52.4 9.7 %gather_fusion = bf16[2048,1024]{1,0:T(8,128)(2,1)} fusion(bf16[1025,1024]{1,0:T(8,128)(2,1)S(1)} %concatenate.15, s32[2048]{0:T(1024)S(1)} %fusion.27), kind=kCustom, calls=%fused_computation | custom fusion | bytes 8396800 | tf_op jit(solution)/shard_map/jit(_take)/gather | solution.py:161
  62.0 2.5 %broadcast_select_fusion = bf16[32,64,1024]{2,1,0:T(8,128)(2,1)S(1)} fusion(bf16[32,64,1024]{2,1,0:T(8,128)(2,1)} %bitcast.17, pred[32,64]{1,0:T(8,128)(4,1)S(1)} %broadcast_in_dim.49), kind=kLoop, calls=%fused_computation.12 | loop fusion | flops 2097152 | bytes 8390656 | tf_op jit(solution)/shard_map/jit(_take)/select_n | solution.py:161
  64.5 100.7 %all_to_all.12 = bf16[32,64,1024]{2,1,0:T(8,128)(2,1)S(1)} all-to-all(bf16[32,64,1024]{2,1,0:T(8,128)(2,1)S(1)} %broadcast_select_fusion), channel_id=1, replica_groups=mesh['win'=8,'band'=4] {'win','band'}, dimensions={0} | all-to-all | bytes 8388608 | tf_op jit(solution)/shard_map/all_to_all | solution.py:162
  165.3 2.3 %copy.11 = bf16[32,64,1024]{2,0,1:T(8,128)(2,1)S(1)} copy(bf16[32,64,1024]{2,1,0:T(8,128)(2,1)S(1)} %all_to_all.12) | data formatting | bytes 8388608 | tf_op jit(solution)/shard_map/all_to_all | solution.py:162
  167.6 4.6 %convolution_bitcast_fusion = f32[2,1024,1024]{2,1,0:T(8,128)S(1)} fusion(bf16[32,2,32,1024]{3,0,2,1:T(8,128)(2,1)S(1)} %bitcast.19), kind=kOutput, calls=%fused_computation.14 | convolution fusion | flops 4294967296 | bytes 12582912 | tf_op jit(solution)/shard_map/sgcm,sgcn->gmn/dot_general | solution.py:164
  172.2 1.0 slice_add_fusion
  173.2 2.1 %select_reduce_fusion = (f32[]{:T(128)}, f32[512,512]{1,0:T(8,128)}) fusion(f32[2,512,512]{2,1,0:T(8,128)S(1)} %get-tuple-element.8, f32[2,512,512]{2,1,0:T(8,128)S(1)} %get-tuple-element.7), kind=kLoop, calls=%fused_computation.37 | loop fusion | flops 1835007 | bytes 5242884 | tf_op jit(solution)/shard_map/jit(trace)/reduce_sum | solution.py:168
  175.3 0.7 broadcast_in_dim.54
  175.9 10.7 %all_to_all.13 = f32[32,1,1]{2,1,0:T(1,128)S(1)} all-to-all(f32[32,1,1]{2,1,0:T(1,128)S(1)} %broadcast_in_dim.54), channel_id=1, replica_groups=mesh['win'=8,'band'=4] {'win','band'}, dimensions={0} | all-to-all | bytes 256 | tf_op jit(solution)/shard_map/all_to_all | solution.py:170
  186.6 0.6 reduce_sum.40
  187.9 0.6 broadcast_in_dim.55.ridge_ref
  188.5 17.6 %factor_rows.1 = f32[512,512]{1,0:T(8,128)} custom-call(f32[8,128]{1,0:T(8,128)} %broadcast_in_dim.55.ridge_ref, f32[512,512]{1,0:T(8,128)} %get-tuple-element.6.fisher_ref), custom_call_target="tpu_custom_call" | custom-call | tf_op jit(solution)/shard_map/factor_rows/pallas_call | solution.py:110
  (9 shorter events, 0.0 us)
Async XLA Ops:
  0.0 23.1 %copy-start = (f32[4,1024]{1,0:T(4,128)S(1)}, f32[4,1024]{1,0:T(4,128)}, u32[]{:S(2)}) copy-start(f32[4,1024]{1,0:T(4,128)} %param.8) | copy-start | bytes 49156
  0.0 23.0 %copy-start.2 = (s32[32]{0:T(128)S(1)}, s32[32]{0:T(128)}, u32[]{:S(2)}) copy-start(s32[32]{0:T(128)} %param.9) | copy-start | bytes 388
  23.1 4.3 %copy-start.1 = (bf16[1024,2,1024]{2,1,0:T(2,128)(2,1)S(1)}, bf16[1024,2,1024]{2,1,0:T(2,128)(2,1)}, u32[]{:S(2)}) copy-start(bf16[1024,2,1024]{2,1,0:T(2,128)(2,1)} %param.5) | copy-start | bytes 12582916

commit v2 on v1

--- a/solution.py
+++ b/solution.py
@@ -1,5 +1,8 @@
+import functools
+
 import jax
 import jax.numpy as jnp
+import numpy as np
 from jax import lax
 from jax.experimental import pallas as pl
 from jax.experimental.pallas import tpu as pltpu
@@ -13,17 +16,6 @@
 ridge_share = 0.1
 
 
-def delay_table():
-    delays = jnp.arange(P_SIZE, dtype=jnp.int32)
-    channel = jnp.arange(FREQ, dtype=jnp.int32)
-    phases = (delays[:, None] * channel[None, :] % FREQ).astype(jnp.float32) * (2.0 * jnp.pi / FREQ)
-    cosine_rows = jnp.cos(phases).astype(jnp.bfloat16).T
-    sine_rows = jnp.sin(phases).astype(jnp.bfloat16).T
-    top_block = jnp.concatenate([cosine_rows, -sine_rows], axis=1)
-    low_block = jnp.concatenate([sine_rows, cosine_rows], axis=1)
-    return jnp.concatenate([top_block, low_block], axis=0)
-
-
 STEP = 16
 LANE = 128
 
@@ -38,9 +30,11 @@
     return lax.dot_general(left, right, (((0,), (0,)), ((), ())), preferred_element_type=jnp.float32)
 
 
-def factor_kernel(ridge_ref, fisher_ref, out_ref, work_ref, left_ref, right_ref):
+def factor_kernel(trace_ref, fisher_ref, out_ref, work_ref, left_ref, right_ref):
     size = fisher_ref.shape[0]
-    ridge = ridge_ref[0:1, 0:1]
+    windows = trace_ref.shape[0]
+    lane_total = jnp.sum(trace_ref[...], axis=0)
+    ridge = jnp.sum(lane_total, axis=1, keepdims=True) * (ridge_share / (windows * size))
     rows = lax.broadcasted_iota(jnp.int32, (STEP, LANE), 0)
     lanes = lax.broadcasted_iota(jnp.int32, (STEP, LANE), 1)
     square_r = lax.broadcasted_iota(jnp.int32, (LANE, LANE), 0)
@@ -105,7 +99,7 @@
             work_ref[mine, rest] = work_ref[mine, rest] - cross(left, right)
 
 
-def factor_rows(fisher, ridge):
+def factor_rows(fisher, traces):
     size = fisher.shape[0]
     return pl.pallas_call(
         factor_kernel,
@@ -118,58 +112,162 @@
             pltpu.VMEM((LANE, size), jnp.bfloat16),
         ],
         name="factor_rows",
-    )(jnp.broadcast_to(ridge, (8, LANE)), fisher)
+    )(traces, fisher)
+
+
+ROWS = 256
+SLOTS = 256
+
+
+def delay_parts():
+    delays = np.arange(P_SIZE, dtype=np.int64)
+    channel = np.arange(FREQ, dtype=np.int64)
+    phases = (channel[:, None] * delays[None, :] % FREQ).astype(np.float32) * np.float32(2.0 * np.pi / FREQ)
+    both = np.concatenate([np.cos(phases), np.sin(phases)], axis=0)
+    return jnp.asarray(both.astype(np.float32)).astype(jnp.bfloat16)
+
+
+def front_kernel(steps, capacity, vis_ref, noise_ref, column_ref, row_ref, pick_ref, bank_ref, table_ref, out_ref, spectra_ref, slot_ref):
+    step = pl.program_id(0)
+    windows = pick_ref.shape[1]
+
+    @pl.when(step < steps)
+    def transform():
+        ids = column_ref[...]
+        lanes = lax.broadcasted_iota(jnp.int32, (ROWS, windows), 1)
+        hit = jnp.broadcast_to(ids // 2, (ROWS, windows)) == lanes
+        picks = jnp.broadcast_to(pick_ref[...], (ROWS, windows))
+        pick = jnp.sum(jnp.where(hit, picks, 0), axis=1, keepdims=True)
+        taper = jnp.broadcast_to(bank_ref[0:1, :], (ROWS, FREQ))
+        for t in range(1, TAPERS):
+            taper = jnp.where(pick == t, bank_ref[t : t + 1, :], taper)
+        weight = taper * noise_ref[...]
+        real = (weight * vis_ref[:, 0, :].astype(jnp.float32)).astype(jnp.bfloat16)
+        imag = (weight * vis_ref[:, 1, :].astype(jnp.float32)).astype(jnp.bfloat16)
+        left = jnp.concatenate(
+            [jnp.concatenate([real, imag], axis=1), jnp.concatenate([imag, -real], axis=1)], axis=0
+        )
+        both = jnp.dot(left, table_ref[...], preferred_element_type=jnp.float32).astype(jnp.bfloat16)
+        here = pl.ds(pl.multiple_of(step * ROWS, ROWS), ROWS)
+        spectra_ref[here, :P_SIZE] = both[:ROWS]
+        spectra_ref[here, P_SIZE:] = both[ROWS:]
+
+    @pl.when(step == 0)
+    def rank():
+        count = row_ref.shape[1]
+        groups = 2 * windows
+        ids = row_ref[...]
+        match = jnp.broadcast_to(ids, (groups, count)) == lax.broadcasted_iota(jnp.int32, (groups, count), 0)
+        first = lax.broadcasted_iota(jnp.int32, (count, count), 0)
+        second = lax.broadcasted_iota(jnp.int32, (count, count), 1)
+        before = jnp.where(first < second, 1.0, 0.0).astype(jnp.bfloat16)
+        member = jnp.where(match, 1.0, 0.0)
+        earlier = jnp.dot(member.astype(jnp.bfloat16), before, preferred_element_type=jnp.float32)
+        order = jnp.sum(member * earlier, axis=0, keepdims=True).astype(jnp.int32)
+        slot_ref[...] = ids * capacity + order
+
+    @pl.when(step >= steps)
+    def place():
+        count = row_ref.shape[1]
+        first = (step - steps) * SLOTS
+        wanted = lax.broadcasted_iota(jnp.int32, (SLOTS, count), 0) + first
+        choose = jnp.where(jnp.broadcast_to(slot_ref[...], (SLOTS, count)) == wanted, 1.0, 0.0).astype(jnp.bfloat16)
+        out_ref[...] = jnp.dot(choose, spectra_ref[...], preferred_element_type=jnp.float32).astype(jnp.bfloat16)
+
+
+def outgoing_slots(vis, inv_noise, assign, taper_bank, taper_pick, windows, capacity):
+    pair_count = assign.shape[0]
+    steps = pair_count // ROWS
+    slots = 2 * windows * capacity
+    last = steps - 1
+
+    def early(step):
+        return jnp.minimum(step, last)
+
+    return pl.pallas_call(
+        functools.partial(front_kernel, steps, capacity),
+        grid=(steps + slots // SLOTS,),
+        out_shape=jax.ShapeDtypeStruct((slots, 2 * P_SIZE), jnp.bfloat16),
+        in_specs=[
+            pl.BlockSpec((ROWS, 2, FREQ), lambda s: (early(s), 0, 0)),
+            pl.BlockSpec((ROWS, FREQ), lambda s: (early(s), 0)),
+            pl.BlockSpec((ROWS, 1), lambda s: (early(s), 0)),
+            pl.BlockSpec((1, pair_count), lambda s: (0, 0)),
+            pl.BlockSpec((1, windows), lambda s: (0, 0)),
+            pl.BlockSpec((TAPERS, FREQ), lambda s: (0, 0)),
+            pl.BlockSpec((2 * FREQ, P_SIZE), lambda s: (0, 0)),
+        ],
+        out_specs=pl.BlockSpec((SLOTS, 2 * P_SIZE), lambda s: (jnp.maximum(s - steps, 0), 0)),
+        scratch_shapes=[
+            pltpu.VMEM((pair_count, 2 * P_SIZE), jnp.bfloat16),
+            pltpu.VMEM((1, pair_count), jnp.int32),
+        ],
+        compiler_params=pltpu.CompilerParams(dimension_semantics=("arbitrary",)),
+        name="front",
+    )(vis, inv_noise, assign[:, None], assign[None, :], taper_pick[None, :], taper_bank, delay_parts())
+
+
+def moment_kernel(rows_ref, fisher_ref, trace_ref, real_ref, imag_ref):
+    sources, capacity, spectral = rows_ref.shape
+    size = spectral // 2
+    rows = rows_ref[...].reshape(sources * capacity, spectral)
+    first, second = rows[:, :size], rows[:, size:]
+    mixed = cross(second, rows)
+    real = cross(first, first) + mixed[:, size:]
+    imag = mixed[:, :size] - mixed[:, :size].T
+
+    @pl.when(pl.program_id(0) == 0)
+    def keep():
+        real_ref[...] = real
+        imag_ref[...] = imag
+
+    @pl.when(pl.program_id(0) == 1)
+    def combine():
+        fisher = 0.5 * (real_ref[...] * real + imag_ref[...] * imag)
+        fisher_ref[...] = fisher
+        square_r = lax.broadcasted_iota(jnp.int32, (LANE, LANE), 0)
+        square_c = lax.broadcasted_iota(jnp.int32, (LANE, LANE), 1)
+        diagonal = jnp.zeros((LANE, LANE), jnp.float32)
+        for p in range(size // LANE):
+            span = slice(LANE * p, LANE * (p + 1))
+            diagonal = diagonal + jnp.where(square_r == square_c, fisher[span, span], 0.0)
+        lanes = jnp.sum(diagonal, axis=0, keepdims=True)
+        trace_ref[...] = jnp.broadcast_to(lanes, trace_ref.shape)
+
+
+def window_moments(incoming, windows):
+    sources, both, spectral = incoming.shape
+    size = spectral // 2
+    capacity = both // 2
+    return pl.pallas_call(
+        moment_kernel,
+        grid=(2,),
+        out_shape=[
+            jax.ShapeDtypeStruct((size, size), jnp.float32),
+            jax.ShapeDtypeStruct((windows, 1, LANE), jnp.float32),
+        ],
+        in_specs=[pl.BlockSpec((sources, capacity, spectral), lambda g: (0, g, 0))],
+        out_specs=[
+            pl.BlockSpec((size, size), lambda g: (0, 0)),
+            pl.BlockSpec((windows, 1, LANE), lambda g: (0, 0, 0)),
+        ],
+        scratch_shapes=[pltpu.VMEM((size, size), jnp.float32)] * 2,
+        compiler_params=pltpu.CompilerParams(dimension_semantics=("arbitrary",)),
+        name="moments",
+    )(incoming)
 
 
 def local(vis, inv_noise, assign, taper_bank, taper_pick):
     win_size = lax.axis_size("win")
     band_size = lax.axis_size("band")
     windows = win_size * band_size
-    pair_count = assign.shape[0]
-    capacity = pair_count // windows
+    capacity = assign.shape[0] // windows
     spectral = 2 * P_SIZE
-    group_lanes = 2 * windows
-    window_ids = assign // 2
-    window_match = (window_ids[:, None] == jnp.arange(windows, dtype=jnp.int32)[None, :]).astype(
-        jnp.int32
-    )
-    picked_taper = jnp.sum(window_match * taper_pick[None, :], axis=1)
-    taper_match = (picked_taper[:, None] == jnp.arange(TAPERS, dtype=jnp.int32)[None, :]).astype(
-        jnp.float32
-    )
-    taper_rows = jnp.dot(
-        taper_match, taper_bank, precision=lax.Precision.HIGHEST, preferred_element_type=jnp.float32
-    )
-    weighted = (taper_rows[:, None, :] * inv_noise[:, None, :] * vis.astype(jnp.float32)).astype(
-        jnp.bfloat16
-    )
-    spectra = jnp.dot(
-        weighted.reshape(pair_count, 2 * FREQ), delay_table(), preferred_element_type=jnp.float32
-    ).astype(jnp.bfloat16)
-    ident_match = (assign[:, None] == jnp.arange(group_lanes, dtype=jnp.int32)[None, :]).astype(
-        jnp.bfloat16
-    )
-    position = jnp.arange(pair_count, dtype=jnp.int32)
-    before = (position[None, :] < position[:, None]).astype(jnp.bfloat16)
-    earlier = jnp.dot(before, ident_match, preferred_element_type=jnp.float32)
-    slot_rank = jnp.sum(earlier * ident_match.astype(jnp.float32), axis=1).astype(jnp.int32)
-    slot_index = assign * capacity + slot_rank
-    source_row = (
-        jnp.full((group_lanes * capacity,), pair_count, jnp.int32).at[slot_index].set(position)
-    )
-    padded = jnp.concatenate([spectra, jnp.zeros((1, spectral), jnp.bfloat16)], axis=0)
-    outgoing = jnp.take(padded, source_row, axis=0)
+    outgoing = outgoing_slots(vis, inv_noise, assign, taper_bank, taper_pick, windows, capacity)
     incoming = lax.all_to_all(outgoing, ("win", "band"), split_axis=0, concat_axis=0, tiled=True)
-    incoming = incoming.reshape(windows, 2, capacity, spectral)
-    moments = jnp.einsum("sgcm,sgcn->gmn", incoming, incoming, preferred_element_type=jnp.float32)
-    real_part = moments[:, :P_SIZE, :P_SIZE] + moments[:, P_SIZE:, P_SIZE:]
-    imag_part = moments[:, P_SIZE:, :P_SIZE] - moments[:, :P_SIZE, P_SIZE:]
-    fisher = 0.5 * (real_part[0] * real_part[1] + imag_part[0] * imag_part[1])
-    local_trace = jnp.trace(fisher)
-    shared = jnp.broadcast_to(local_trace, (windows,))
-    diag_total = jnp.sum(lax.all_to_all(shared, ("win", "band"), 0, 0, tiled=True))
-    ridge_term = ridge_share * diag_total / (windows * P_SIZE)
-    return factor_rows(fisher, ridge_term)[None]
+    fisher, traces = window_moments(incoming.reshape(windows, 2 * capacity, spectral), windows)
+    traces = lax.all_to_all(traces, ("win", "band"), split_axis=0, concat_axis=0, tiled=True)
+    return factor_rows(fisher, traces)[None]
 
 
 def solution(mesh):

time: 206 us -> 157 us (0.76)
  matrix products: 29.1 us -> 0 us
  other arithmetic: 28 us -> 0 us
  Pallas kernels: 17.6 us -> 42.7 us
  local copies, waits for them, and re-layouts: 19.3 us -> 1.71 us
    dot_general x4 -> x0, matrix products: 29.1 us -> none  [the longest x1 18.9 us: local(): jnp.dot(weighted.reshape(pair_count, 2 * FREQ), delay_table(), preferred_...]
    pallas_call x0 -> x2, Pallas kernels: none -> 25 us  [the longest x1 18.5 us: outgoing_slots(): pl.pallas_call(functools.partial(front_kernel, steps, capacity), grid=(st...]
    convert_element_type x2 -> x0, other arithmetic: 12.9 us -> none  [the longest x1 8.48 us: delay_table(): sine_rows = jnp.sin(phases).astype(jnp.bfloat16).T]
    gather x1 -> x0, local copies, waits for them, and re-layouts: 9.67 us -> none  [local(): outgoing = jnp.take(padded, source_row, axis=0)]
    neg x1 -> x0, other arithmetic: 7.98 us -> none  [delay_table(): top_block = jnp.concatenate([cosine_rows, -sine_rows], axis=1)]
    scatter x1 -> x0, local copies, waits for them, and re-layouts: 4.32 us -> none  [local(): jnp.full((group_lanes * capacity,), pair_count, jnp.int32).at[slot_index]]
    select_n x2 -> x0, other arithmetic: 3.21 us -> none  [the longest x1 2.51 us: local(): outgoing = jnp.take(padded, source_row, axis=0)]
    reduce_sum x3 -> x0, other arithmetic: 2.8 us -> none  [the longest x1 2.08 us: local(): local_trace = jnp.trace(fisher)]
where the time goes in v2:
time: 157 us; the launch traced here: 156 us
  blocking collectives  112 us (71%)
  Pallas kernels  42.7 us (27%)
  local copies, waits for them, and re-layouts  1.71 us (1%)
    all_to_all x1, blocking collectives, local(): lax.all_to_all(outgoing, ('win', 'band'), split_axis=0, concat_axis=0, ti...  101 us
    pallas_call x1, Pallas kernels, outgoing_slots(): pl.pallas_call(functools.partial(front_kernel, steps, capacity), grid=(st...  18.5 us
    pallas_call x1, Pallas kernels, factor_rows(): pl.pallas_call(factor_kernel, out_shape=jax.ShapeDtypeStruct((size, size)...  17.7 us
    all_to_all x1, blocking collectives, local(): lax.all_to_all(traces, ('win', 'band'), split_axis=0, concat_axis=0, tile...  10.9 us
    pallas_call x1, Pallas kernels, window_moments(): pl.pallas_call(moment_kernel, grid=(2,), out_shape=[jax.ShapeDtypeStruct(...  6.56 us

profile of v2, /device:TPU:0, one launch (start us, length us, event | category | flops | bytes accessed | tf_op | source)
XLA Modules:
  0.0 156.4 jit_solution(7556696554333924353)
XLA Ops:
  0.0 1.7 %copy.7.column_ref = s32[1024,1]{1,0:T(8,128)} copy(s32[1024,1]{0,1:T(1,128)} %bitcast.6) | data formatting | bytes 8192 | tf_op jit(solution)/shard_map/broadcast_in_dim | solution.py:207
  1.7 18.5 %front.1 = bf16[2048,1024]{1,0:T(8,128)(2,1)} custom-call(bf16[1024,2,1024]{2,1,0:T(2,128)(2,1)} %vis_ref.1, f32[1024,1024]{1,0:T(8,128)} %noise_ref.1, s32[1024,1]{1,0:T(8,128)} %copy.7.column_ref, s32[1,1024]{1,0:T(1,128)} %bitcast.7, s32[1,32]{1,0:T(1,128)} %bitcast.8, f32[4,1024]{1,0:T(4,128)} %bank_ref.1, bf16[2048,512]{1,0:T(8,128)(2,1)} %constant.3.table_ref), custom_call_target="tpu_custom_call" | custom-call | tf_op jit(solution)/shard_map/front/pallas_call | solution.py:187
  20.2 101.1 %all_to_all.14.rows_ref = bf16[32,64,1024]{2,1,0:T(8,128)(2,1)} all-to-all(bf16[32,64,1024]{2,1,0:T(8,128)(2,1)} %bitcast.5), channel_id=1, replica_groups=mesh['win'=8,'band'=4] {'win','band'}, dimensions={0} | all-to-all | bytes 8388608 | tf_op jit(solution)/shard_map/all_to_all | solution.py:267
  121.2 6.6 %moments.1 = (f32[512,512]{1,0:T(8,128)}, f32[32,1,128]{2,1,0:T(1,128)}) custom-call(bf16[32,64,1024]{2,1,0:T(8,128)(2,1)} %all_to_all.14.rows_ref), custom_call_target="tpu_custom_call" | custom-call | tf_op jit(solution)/shard_map/moments/pallas_call | solution.py:242
  127.8 10.9 %all_to_all.15.trace_ref = f32[32,1,128]{2,1,0:T(1,128)} all-to-all(f32[32,1,128]{2,1,0:T(1,128)} %get-tuple-element.7), channel_id=1, replica_groups=mesh['win'=8,'band'=4] {'win','band'}, dimensions={0} | all-to-all | bytes 32768 | tf_op jit(solution)/shard_map/all_to_all | solution.py:269
  138.7 17.7 %factor_rows.1 = f32[512,512]{1,0:T(8,128)} custom-call(f32[32,1,128]{2,1,0:T(1,128)} %all_to_all.15.trace_ref, f32[512,512]{1,0:T(8,128)} %get-tuple-element.8.fisher_ref), custom_call_target="tpu_custom_call" | custom-call | tf_op jit(solution)/shard_map/factor_rows/pallas_call | solution.py:104

commit v3 on v2

--- a/solution.py
+++ b/solution.py
@@ -30,8 +30,8 @@
     return lax.dot_general(left, right, (((0,), (0,)), ((), ())), preferred_element_type=jnp.float32)
 
 
-def factor_kernel(trace_ref, fisher_ref, out_ref, work_ref, left_ref, right_ref):
-    size = fisher_ref.shape[0]
+def factor_kernel(trace_ref, near_ref, far_first_ref, far_second_ref, out_ref, work_ref, left_ref, right_ref):
+    size = out_ref.shape[0]
     windows = trace_ref.shape[0]
     lane_total = jnp.sum(trace_ref[...], axis=0)
     ridge = jnp.sum(lane_total, axis=1, keepdims=True) * (ridge_share / (windows * size))
@@ -39,12 +39,20 @@
     lanes = lax.broadcasted_iota(jnp.int32, (STEP, LANE), 1)
     square_r = lax.broadcasted_iota(jnp.int32, (LANE, LANE), 0)
     square_c = lax.broadcasted_iota(jnp.int32, (LANE, LANE), 1)
-    eye = jnp.where(square_r == square_c, jnp.broadcast_to(ridge, (LANE, LANE)), 0.0)
+    ridges = jnp.broadcast_to(ridge, (LANE, LANE))
+
+    def product(p, q):
+        mine, across = slice(LANE * p, LANE * (p + 1)), slice(LANE * q, LANE * (q + 1))
+        first = near_ref[0, mine, across] + far_first_ref[0, mine, across].astype(jnp.float32)
+        second = near_ref[1, mine, across] + far_second_ref[0, mine, across].astype(jnp.float32)
+        return 0.5 * first * second
+
     for p in range(size // LANE):
-        base = p * LANE
-        tail = slice(base, base + LANE)
-        work_ref[tail, base:] = fisher_ref[tail, base:]
-        work_ref[tail, tail] = fisher_ref[tail, tail] + eye
+        mine = slice(LANE * p, LANE * (p + 1))
+        block = product(p, p)
+        work_ref[mine, mine] = jnp.where(square_r == square_c, block + ridges, block + block.T)
+        for q in range(p + 1, size // LANE):
+            work_ref[mine, LANE * q : LANE * (q + 1)] = product(p, q) + product(q, p).T
     for p in range(size // LANE):
         base = p * LANE
         tiles = (size - base) // LANE
@@ -99,12 +107,12 @@
             work_ref[mine, rest] = work_ref[mine, rest] - cross(left, right)
 
 
-def factor_rows(fisher, traces):
-    size = fisher.shape[0]
+def factor_rows(traces, near, first, second):
+    size = near.shape[1]
     return pl.pallas_call(
         factor_kernel,
         out_shape=jax.ShapeDtypeStruct((size, size), jnp.float32),
-        in_specs=[pl.BlockSpec(memory_space=pltpu.VMEM)] * 2,
+        in_specs=[pl.BlockSpec(memory_space=pltpu.VMEM)] * 4,
         out_specs=pl.BlockSpec(memory_space=pltpu.VMEM),
         scratch_shapes=[
             pltpu.VMEM((size, size), jnp.float32),
@@ -112,28 +120,37 @@
             pltpu.VMEM((LANE, size), jnp.bfloat16),
         ],
         name="factor_rows",
-    )(traces, fisher)
+    )(traces, near, first, second)
 
 
 ROWS = 256
-SLOTS = 256
+SLOTS = 512
 
 
 def delay_parts():
     delays = np.arange(P_SIZE, dtype=np.int64)
-    channel = np.arange(FREQ, dtype=np.int64)
+    channel = np.arange(FREQ // 2, dtype=np.int64)
     phases = (channel[:, None] * delays[None, :] % FREQ).astype(np.float32) * np.float32(2.0 * np.pi / FREQ)
     both = np.concatenate([np.cos(phases), np.sin(phases)], axis=0)
     return jnp.asarray(both.astype(np.float32)).astype(jnp.bfloat16)
 
 
-def front_kernel(steps, capacity, vis_ref, noise_ref, column_ref, row_ref, pick_ref, bank_ref, table_ref, out_ref, spectra_ref, slot_ref):
+def front_kernel(steps, capacity, quarter, vis_ref, noise_ref, part_ref, row_ref, pick_ref, bank_ref, parts_ref, first_ref, second_ref, spectra_ref, slot_ref, table_ref):
     step = pl.program_id(0)
     windows = pick_ref.shape[1]
 
+    @pl.when(step == 0)
+    def fill():
+        near = FREQ // 2
+        odd = lax.broadcasted_iota(jnp.int32, (near, P_SIZE), 1) & 1
+        for t in range(2):
+            part = parts_ref[near * t : near * (t + 1), :]
+            table_ref[FREQ * t : FREQ * t + near, :] = part
+            table_ref[FREQ * t + near : FREQ * (t + 1), :] = jnp.where(odd == 1, -part, part)
+
     @pl.when(step < steps)
     def transform():
-        ids = column_ref[...]
+        ids = jnp.broadcast_to(part_ref[...], (8, ROWS)).T[:, 0:1]
         lanes = lax.broadcasted_iota(jnp.int32, (ROWS, windows), 1)
         hit = jnp.broadcast_to(ids // 2, (ROWS, windows)) == lanes
         picks = jnp.broadcast_to(pick_ref[...], (ROWS, windows))
@@ -156,105 +173,164 @@
     def rank():
         count = row_ref.shape[1]
         groups = 2 * windows
-        ids = row_ref[...]
-        match = jnp.broadcast_to(ids, (groups, count)) == lax.broadcasted_iota(jnp.int32, (groups, count), 0)
+        names = row_ref[...]
+        match = jnp.broadcast_to(names, (groups, count)) == lax.broadcasted_iota(jnp.int32, (groups, count), 0)
         first = lax.broadcasted_iota(jnp.int32, (count, count), 0)
         second = lax.broadcasted_iota(jnp.int32, (count, count), 1)
         before = jnp.where(first < second, 1.0, 0.0).astype(jnp.bfloat16)
         member = jnp.where(match, 1.0, 0.0)
         earlier = jnp.dot(member.astype(jnp.bfloat16), before, preferred_element_type=jnp.float32)
         order = jnp.sum(member * earlier, axis=0, keepdims=True).astype(jnp.int32)
-        slot_ref[...] = ids * capacity + order
-
-    @pl.when(step >= steps)
-    def place():
-        count = row_ref.shape[1]
-        first = (step - steps) * SLOTS
-        wanted = lax.broadcasted_iota(jnp.int32, (SLOTS, count), 0) + first
-        choose = jnp.where(jnp.broadcast_to(slot_ref[...], (SLOTS, count)) == wanted, 1.0, 0.0).astype(jnp.bfloat16)
-        out_ref[...] = jnp.dot(choose, spectra_ref[...], preferred_element_type=jnp.float32).astype(jnp.bfloat16)
-
-
-def outgoing_slots(vis, inv_noise, assign, taper_bank, taper_pick, windows, capacity):
+        upper = lax.axis_index("win") * 2 >= lax.axis_size("win")
+        shifted = jnp.where(names >= windows, names - windows, names + windows)
+        ordered = jnp.where(upper, names, shifted)
+        split = ((ordered & 1) * (windows // 2) + ordered // 2) * capacity
+        slot_ref[...] = jnp.where(ordered < windows, split, ordered * capacity) + order
+
+    @pl.when((step >= steps) & (step < steps + quarter))
+    def first():
+        first_ref[...] = placed_rows((step - steps) * SLOTS, slot_ref, spectra_ref)
+
+    @pl.when(step >= steps + quarter)
+    def second():
+        second_ref[...] = placed_rows((step - steps) * SLOTS, slot_ref, spectra_ref)
+
+
+def placed_rows(first, slot_ref, spectra_ref):
+    count = slot_ref.shape[1]
+    wanted = lax.broadcasted_iota(jnp.int32, (SLOTS, count), 0) + first
+    choose = jnp.where(jnp.broadcast_to(slot_ref[...], (SLOTS, count)) == wanted, 1.0, 0.0).astype(jnp.bfloat16)
+    return jnp.dot(choose, spectra_ref[...], preferred_element_type=jnp.float32).astype(jnp.bfloat16)
+
+
+def near_kernel(offset, slot_ref, spectra_ref, out_ref):
+    out_ref[...] = placed_rows(offset + pl.program_id(0) * SLOTS, slot_ref, spectra_ref)
+
+
+def near_slots(slots, spectra, offset):
+    count, spectral = spectra.shape
+    return pl.pallas_call(
+        functools.partial(near_kernel, offset),
+        grid=(offset // SLOTS,),
+        out_shape=jax.ShapeDtypeStruct((offset, spectral), jnp.bfloat16),
+        in_specs=[pl.BlockSpec((1, count), lambda s: (0, 0)), pl.BlockSpec((count, spectral), lambda s: (0, 0))],
+        out_specs=pl.BlockSpec((SLOTS, spectral), lambda s: (s, 0)),
+        name="near",
+    )(slots, spectra)
+
+
+def far_slots(vis, inv_noise, assign, taper_bank, taper_pick, windows, capacity):
     pair_count = assign.shape[0]
     steps = pair_count // ROWS
-    slots = 2 * windows * capacity
+    slots = windows * capacity // 2
+    quarter = slots // SLOTS
     last = steps - 1
+    names = assign[None, :]
 
     def early(step):
         return jnp.minimum(step, last)
 
     return pl.pallas_call(
-        functools.partial(front_kernel, steps, capacity),
-        grid=(steps + slots // SLOTS,),
-        out_shape=jax.ShapeDtypeStruct((slots, 2 * P_SIZE), jnp.bfloat16),
+        functools.partial(front_kernel, steps, capacity, quarter),
+        grid=(steps + 2 * quarter,),
+        out_shape=[
+            jax.ShapeDtypeStruct((slots, 2 * P_SIZE), jnp.bfloat16),
+            jax.ShapeDtypeStruct((slots, 2 * P_SIZE), jnp.bfloat16),
+            jax.ShapeDtypeStruct((pair_count, 2 * P_SIZE), jnp.bfloat16),
+            jax.ShapeDtypeStruct((1, pair_count), jnp.int32),
+        ],
         in_specs=[
             pl.BlockSpec((ROWS, 2, FREQ), lambda s: (early(s), 0, 0)),
             pl.BlockSpec((ROWS, FREQ), lambda s: (early(s), 0)),
-            pl.BlockSpec((ROWS, 1), lambda s: (early(s), 0)),
+            pl.BlockSpec((1, ROWS), lambda s: (0, early(s))),
             pl.BlockSpec((1, pair_count), lambda s: (0, 0)),
             pl.BlockSpec((1, windows), lambda s: (0, 0)),
             pl.BlockSpec((TAPERS, FREQ), lambda s: (0, 0)),
-            pl.BlockSpec((2 * FREQ, P_SIZE), lambda s: (0, 0)),
-        ],
-        out_specs=pl.BlockSpec((SLOTS, 2 * P_SIZE), lambda s: (jnp.maximum(s - steps, 0), 0)),
-        scratch_shapes=[
-            pltpu.VMEM((pair_count, 2 * P_SIZE), jnp.bfloat16),
-            pltpu.VMEM((1, pair_count), jnp.int32),
-        ],
+            pl.BlockSpec((FREQ, P_SIZE), lambda s: (0, 0)),
+        ],
+        out_specs=[
+            pl.BlockSpec((SLOTS, 2 * P_SIZE), lambda s: (jnp.clip(s - steps, 0, quarter - 1), 0)),
+            pl.BlockSpec((SLOTS, 2 * P_SIZE), lambda s: (jnp.maximum(s - steps - quarter, 0), 0)),
+            pl.BlockSpec((pair_count, 2 * P_SIZE), lambda s: (0, 0)),
+            pl.BlockSpec((1, pair_count), lambda s: (0, 0)),
+        ],
+        scratch_shapes=[pltpu.VMEM((2 * FREQ, P_SIZE), jnp.bfloat16)],
         compiler_params=pltpu.CompilerParams(dimension_semantics=("arbitrary",)),
         name="front",
-    )(vis, inv_noise, assign[:, None], assign[None, :], taper_pick[None, :], taper_bank, delay_parts())
-
-
-def moment_kernel(rows_ref, fisher_ref, trace_ref, real_ref, imag_ref):
-    sources, capacity, spectral = rows_ref.shape
+    )(vis, inv_noise, names, names, taper_pick[None, :], taper_bank, delay_parts())
+
+
+def packed_moments(rows):
+    sources, capacity, spectral = rows.shape
     size = spectral // 2
-    rows = rows_ref[...].reshape(sources * capacity, spectral)
+    rows = rows.reshape(sources * capacity, spectral)
     first, second = rows[:, :size], rows[:, size:]
     mixed = cross(second, rows)
     real = cross(first, first) + mixed[:, size:]
     imag = mixed[:, :size] - mixed[:, :size].T
+    r = lax.broadcasted_iota(jnp.int32, (size, size), 0)
+    c = lax.broadcasted_iota(jnp.int32, (size, size), 1)
+    packed = jnp.where(r <= c, real, imag)
+    return packed, jnp.sum(jnp.where(r == c, real, 0.0), axis=0, keepdims=True)
+
+
+def far_kernel(rows_ref, packed_ref, power_ref):
+    packed, power = packed_moments(rows_ref[...])
+    packed_ref[0] = packed.astype(jnp.bfloat16)
+    power_ref[0] = power
+
+
+def near_moment_kernel(rows_ref, first_ref, second_ref, packed_ref, trace_ref, power_ref):
+    packed, power = packed_moments(rows_ref[...])
+    packed_ref[0] = packed
+    total = power + jnp.where(pl.program_id(0) == 0, first_ref[0], second_ref[0])
 
     @pl.when(pl.program_id(0) == 0)
     def keep():
-        real_ref[...] = real
-        imag_ref[...] = imag
+        power_ref[...] = total
 
     @pl.when(pl.program_id(0) == 1)
     def combine():
-        fisher = 0.5 * (real_ref[...] * real + imag_ref[...] * imag)
-        fisher_ref[...] = fisher
-        square_r = lax.broadcasted_iota(jnp.int32, (LANE, LANE), 0)
-        square_c = lax.broadcasted_iota(jnp.int32, (LANE, LANE), 1)
-        diagonal = jnp.zeros((LANE, LANE), jnp.float32)
-        for p in range(size // LANE):
-            span = slice(LANE * p, LANE * (p + 1))
-            diagonal = diagonal + jnp.where(square_r == square_c, fisher[span, span], 0.0)
-        lanes = jnp.sum(diagonal, axis=0, keepdims=True)
+        both = 0.5 * power_ref[...] * total
+        lanes = both[:, :LANE]
+        for t in range(1, both.shape[1] // LANE):
+            lanes = lanes + both[:, LANE * t : LANE * (t + 1)]
         trace_ref[...] = jnp.broadcast_to(lanes, trace_ref.shape)
 
 
-def window_moments(incoming, windows):
+def far_moments(incoming):
+    _, _, spectral = incoming.shape
+    size = spectral // 2
+    return pl.pallas_call(
+        far_kernel,
+        out_shape=[
+            jax.ShapeDtypeStruct((1, size, size), jnp.bfloat16),
+            jax.ShapeDtypeStruct((1, 1, size), jnp.float32),
+        ],
+        name="far_moments",
+    )(incoming)
+
+
+def near_moments(incoming, first, second, windows):
     sources, both, spectral = incoming.shape
     size = spectral // 2
-    capacity = both // 2
-    return pl.pallas_call(
-        moment_kernel,
+    power = pl.BlockSpec((1, 1, size), lambda g: (0, 0, 0))
+    return pl.pallas_call(
+        near_moment_kernel,
         grid=(2,),
         out_shape=[
-            jax.ShapeDtypeStruct((size, size), jnp.float32),
+            jax.ShapeDtypeStruct((2, size, size), jnp.float32),
             jax.ShapeDtypeStruct((windows, 1, LANE), jnp.float32),
         ],
-        in_specs=[pl.BlockSpec((sources, capacity, spectral), lambda g: (0, g, 0))],
+        in_specs=[pl.BlockSpec((sources, both // 2, spectral), lambda g: (0, g, 0)), power, power],
         out_specs=[
-            pl.BlockSpec((size, size), lambda g: (0, 0)),
+            pl.BlockSpec((1, size, size), lambda g: (g, 0, 0)),
             pl.BlockSpec((windows, 1, LANE), lambda g: (0, 0, 0)),
         ],
-        scratch_shapes=[pltpu.VMEM((size, size), jnp.float32)] * 2,
+        scratch_shapes=[pltpu.VMEM((1, size), jnp.float32)],
         compiler_params=pltpu.CompilerParams(dimension_semantics=("arbitrary",)),
-        name="moments",
-    )(incoming)
+        name="near_moments",
+    )(incoming, first, second)
 
 
 def local(vis, inv_noise, assign, taper_bank, taper_pick):
@@ -263,11 +339,29 @@
     windows = win_size * band_size
     capacity = assign.shape[0] // windows
     spectral = 2 * P_SIZE
-    outgoing = outgoing_slots(vis, inv_noise, assign, taper_bank, taper_pick, windows, capacity)
-    incoming = lax.all_to_all(outgoing, ("win", "band"), split_axis=0, concat_axis=0, tiled=True)
-    fisher, traces = window_moments(incoming.reshape(windows, 2 * capacity, spectral), windows)
-    traces = lax.all_to_all(traces, ("win", "band"), split_axis=0, concat_axis=0, tiled=True)
-    return factor_rows(fisher, traces)[None]
+    half = windows // 2
+    groups = [list(range(half)), list(range(half, windows))]
+    mirror = [(i, (i + half) % windows) for i in range(windows)]
+    everywhere = ("win", "band")
+
+    def gather_half(rows):
+        rows = rows.reshape(half, rows.shape[0] // half, spectral)
+        return lax.all_to_all(
+            rows, everywhere, split_axis=0, concat_axis=0, axis_index_groups=groups, tiled=True
+        )
+
+    *fars, spectra, slots = far_slots(vis, inv_noise, assign, taper_bank, taper_pick, windows, capacity)
+    near = near_slots(slots, spectra, windows * capacity)
+    received, powers = [], []
+    for far in fars:
+        far = gather_half(far)
+        packed, power = far_moments(far)
+        powers.append(lax.ppermute(power, everywhere, mirror))
+        received.append(lax.ppermute(packed, everywhere, mirror))
+    near = gather_half(near)
+    near, traces = near_moments(near, *powers, windows)
+    traces = lax.all_to_all(traces, everywhere, split_axis=0, concat_axis=0, tiled=True)
+    return factor_rows(traces, near, *received)[None]
 
 
 def solution(mesh):

time: 157 us -> 155 us (0.987)
  blocking collectives: 112 us -> 22.6 us
  waiting for transfers between devices: 0 us -> 58.2 us
  starting transfers between devices: 0 us -> 19.3 us
  Pallas kernels: 42.7 us -> 50.9 us
  local copies, waits for them, and re-layouts: 1.71 us -> 3.47 us
    all_to_all x2 -> x1, blocking collectives: 112 us -> 22.6 us  [gather_half(): lax.all_to_all(rows, everywhere, split_axis=0, concat_axis=0, axis_index_...]
    ppermute x0 -> x4, waiting for transfers between devices: none -> 40.3 us  [the longest x2 40.3 us: local(): powers.append(lax.ppermute(power, everywhere, mirror))]
    all_to_all x0 -> x3, waiting for transfers between devices: none -> 18 us  [the longest x2 11 us: gather_half(): lax.all_to_all(rows, everywhere, split_axis=0, concat_axis=0, axis_index_...]
    all_to_all x0 -> x3, starting transfers between devices: none -> 13.5 us  [the longest x2 7.37 us: gather_half(): lax.all_to_all(rows, everywhere, split_axis=0, concat_axis=0, axis_index_...]
    pallas_call x2 -> x5, Pallas kernels: 25 us -> 32.6 us  [the longest x1 17 us: far_slots(): pl.pallas_call(functools.partial(front_kernel, steps, capacity, quarter),...]
    ppermute x0 -> x4, starting transfers between devices: none -> 5.85 us  [the longest x2 2.93 us: local(): received.append(lax.ppermute(packed, everywhere, mirror))]
    unnamed x0 -> x14, local copies, waits for them, and re-layouts: none -> 3.47 us
    broadcast_in_dim x1 -> x0, local copies, waits for them, and re-layouts: 1.71 us -> none  [outgoing_slots(): assign[:, None]]
  transfers between devices with their start and end apart: 0 -> 7, of which waited for: 0 -> 3; matrix products, arithmetic and copies ran while one was open for 0% -> 0% of each run, Pallas kernels for 0% -> 10%
where the time goes in v3:
time: 155 us
  waiting for transfers between devices  58.2 us (38%)
  Pallas kernels  50.9 us (33%)
  blocking collectives  22.6 us (15%)
  starting transfers between devices  19.3 us (12%)
  local copies, waits for them, and re-layouts  3.47 us (2%)
    ppermute x2, waiting for transfers between devices, local(): powers.append(lax.ppermute(power, everywhere, mirror))  40.3 us
    all_to_all x1, blocking collectives, gather_half(): lax.all_to_all(rows, everywhere, split_axis=0, concat_axis=0, axis_index_...  22.6 us
    pallas_call x1, Pallas kernels, factor_rows(): pl.pallas_call(factor_kernel, out_shape=jax.ShapeDtypeStruct((size, size)...  18.3 us
    pallas_call x1, Pallas kernels, far_slots(): pl.pallas_call(functools.partial(front_kernel, steps, capacity, quarter),...  17 us
    all_to_all x2, waiting for transfers between devices, gather_half(): lax.all_to_all(rows, everywhere, split_axis=0, concat_axis=0, axis_index_...  11 us
    all_to_all x2, starting transfers between devices, gather_half(): lax.all_to_all(rows, everywhere, split_axis=0, concat_axis=0, axis_index_...  7.37 us
    all_to_all x1, waiting for transfers between devices, local(): lax.all_to_all(traces, everywhere, split_axis=0, concat_axis=0, tiled=True)  6.95 us
    all_to_all x1, starting transfers between devices, local(): lax.all_to_all(traces, everywhere, split_axis=0, concat_axis=0, tiled=True)  6.12 us
  transfers between devices with their start and end apart: 7, of which 3 were waited for; matrix products, arithmetic and copies ran while one was open for 0% of the time, Pallas kernels for 10%

profile of v3, /device:TPU:0, one launch (start us, length us, event | category | flops | bytes accessed | tf_op | source)
XLA Modules:
  0.0 154.6 jit_solution(16931931023767383325)
XLA Ops:
  0.0 17.0 %front.1 = (bf16[512,1024]{1,0:T(8,128)(2,1)}, bf16[512,1024]{1,0:T(8,128)(2,1)}, bf16[1024,1024]{1,0:T(8,128)(2,1)}, s32[1,1024]{1,0:T(1,128)}) custom-call(bf16[1024,2,1024]{2,1,0:T(2,128)(2,1)} %vis_ref.1, f32[1024,1024]{1,0:T(8,128)} %noise_ref.1, s32[1,1024]{1,0:T(1,128)} %bitcast.8, s32[1,1024]{1,0:T(1,128)} %bitcast.9, s32[1,32]{1,0:T(1,128)} %bitcast.10, ...), custom_call_target="tpu_custom_call" | custom-call | tf_op jit(solution)/shard_map/front/pallas_call | solution.py:233
  17.0 22.6 %all_to_all.20.rows_ref = bf16[16,32,1024]{2,1,0:T(8,128)(2,1)} all-to-all(bf16[16,32,1024]{2,1,0:T(8,128)(2,1)} %bitcast.7), channel_id=1, replica_groups={{0,1,2,3,4,5,6,7,8,9,10,11,12,13,14,15},{16,17,18,19,20,21,22,23,24,25,..., dimensions={0} | all-to-all | bytes 2097152 | tf_op jit(solution)/shard_map/all_to_all | solution.py:349
  39.6 3.7 %all-to-all-start.2 = ((bf16[16,32,1024]{2,1,0:T(8,128)(2,1)}), bf16[16,32,1024]{2,1,0:T(8,128)(2,1)S(1)}, u32[]{:S(2)}, u32[]{:S(2)}) async-start(bf16[16,32,1024]{2,1,0:T(8,128)(2,1)} %bitcast.4), calls=%async_computation.2 | async-start | bytes 2097152 | tf_op jit(solution)/shard_map/all_to_all | solution.py:349
  43.3 5.1 %near.1 = bf16[1024,1024]{1,0:T(8,128)(2,1)} custom-call(s32[1,1024]{1,0:T(1,128)} %get-tuple-element.15.slot_ref, bf16[1024,1024]{1,0:T(8,128)(2,1)} %get-tuple-element.16.spectra_ref), custom_call_target="tpu_custom_call" | custom-call | tf_op jit(solution)/shard_map/near/pallas_call | solution.py:212
  48.4 11.0 %all-to-all-done.2.rows_ref = bf16[16,32,1024]{2,1,0:T(8,128)(2,1)S(1)} async-done(((bf16[16,32,1024]{2,1,0:T(8,128)(2,1)}), bf16[16,32,1024]{2,1,0:T(8,128)(2,1)S(1)}, u32[]{:S(2)}, u32[]{:S(2)}) %all-to-all-start.2) | async-done | bytes 1048608 | tf_op jit(solution)/shard_map/all_to_all | solution.py:349
  59.4 1.0 copy-done.1
  60.4 3.7 %all-to-all-start = ((bf16[16,64,1024]{2,1,0:T(8,128)(2,1)}), bf16[16,64,1024]{2,1,0:T(8,128)(2,1)S(1)}, u32[]{:S(2)}, u32[]{:S(2)}) async-start(bf16[16,64,1024]{2,1,0:T(8,128)(2,1)} %bitcast.6), calls=%async_computation | async-start | bytes 4194304 | tf_op jit(solution)/shard_map/all_to_all | solution.py:349
  64.1 3.1 %far_moments.3 = (bf16[1,512,512]{2,1,0:T(8,128)(2,1)}, f32[1,1,512]{2,1,0:T(1,128)}) custom-call(bf16[16,32,1024]{2,1,0:T(8,128)(2,1)} %copy-done.1), custom_call_target="tpu_custom_call" | custom-call | tf_op jit(solution)/shard_map/far_moments/pallas_call | solution.py:304
  67.2 2.6 %collective-permute-start.3 = (bf16[1,512,512]{2,1,0:T(8,128)(2,1)}, bf16[1,512,512]{2,1,0:T(8,128)(2,1)S(1)}, u32[]{:S(2)}, u32[]{:S(2)}) collective-permute-start(bf16[1,512,512]{2,1,0:T(8,128)(2,1)} %get-tuple-element.24), channel_id=1, source_target_pairs={{0,16},{1,17},{2,18},{3,19},{4,20},{5,21},{6,22},{7,23},{8,24},{9,... | collective-permute-start | bytes 1572872 | tf_op jit(solution)/shard_map/ppermute | solution.py:360
  69.8 3.0 %far_moments.2 = (bf16[1,512,512]{2,1,0:T(8,128)(2,1)}, f32[1,1,512]{2,1,0:T(1,128)}) custom-call(bf16[16,32,1024]{2,1,0:T(8,128)(2,1)} %all_to_all.20.rows_ref), custom_call_target="tpu_custom_call" | custom-call | tf_op jit(solution)/shard_map/far_moments/pallas_call | solution.py:304
  72.8 0.3 collective-permute-start.2
  73.1 2.6 %collective-permute-start.1 = (f32[1,1,512]{2,1,0:T(1,128)}, f32[1,1,512]{2,1,0:T(1,128)S(1)}, u32[]{:S(2)}, u32[]{:S(2)}) collective-permute-start(f32[1,1,512]{2,1,0:T(1,128)} %get-tuple-element.20), channel_id=1, source_target_pairs={{0,16},{1,17},{2,18},{3,19},{4,20},{5,21},{6,22},{7,23},{8,24},{9,... | collective-permute-start | bytes 6152 | tf_op jit(solution)/shard_map/ppermute | solution.py:359
  75.7 0.3 collective-permute-start
  76.1 40.2 %collective-permute-done.1.second_ref = f32[1,1,512]{2,1,0:T(1,128)S(1)} collective-permute-done((f32[1,1,512]{2,1,0:T(1,128)}, f32[1,1,512]{2,1,0:T(1,128)S(1)}, u32[]{:S(2)}, u32[]{:S(2)}) %collective-permute-start.1) | collective-permute-done | bytes 2080 | tf_op jit(solution)/shard_map/ppermute | solution.py:359
  116.3 0.0 collective-permute-done.first_ref
  116.3 0.0 all-to-all-done.rows_ref
  116.3 0.6 copy-done.5
  116.9 0.0 copy-done.6
  116.9 1.3 copy-done
  118.2 4.4 %near_moments.1 = (f32[2,512,512]{2,1,0:T(8,128)}, f32[32,1,128]{2,1,0:T(1,128)}) custom-call(bf16[16,64,1024]{2,1,0:T(8,128)(2,1)} %copy-done, f32[1,1,512]{2,1,0:T(1,128)} %copy-done.6, f32[1,1,512]{2,1,0:T(1,128)} %copy-done.5), custom_call_target="tpu_custom_call" | custom-call | tf_op jit(solution)/shard_map/near_moments/pallas_call | solution.py:318
  122.6 6.1 %all-to-all-start.3 = ((f32[32,1,128]{2,1,0:T(1,128)}), f32[32,1,128]{2,1,0:T(1,128)S(1)}, u32[]{:S(2)}, u32[]{:S(2)}) async-start(f32[32,1,128]{2,1,0:T(1,128)} %get-tuple-element.21), calls=%async_computation.3 | async-start | bytes 32768 | tf_op jit(solution)/shard_map/all_to_all | solution.py:363
  128.7 7.0 %all-to-all-done.3.trace_ref = f32[32,1,128]{2,1,0:T(1,128)S(1)} async-done(((f32[32,1,128]{2,1,0:T(1,128)}), f32[32,1,128]{2,1,0:T(1,128)S(1)}, u32[]{:S(2)}, u32[]{:S(2)}) %all-to-all-start.3) | async-done | bytes 16416 | tf_op jit(solution)/shard_map/all_to_all | solution.py:363
  135.7 0.6 copy-done.4
  136.3 18.3 %factor_rows.1 = f32[512,512]{1,0:T(8,128)} custom-call(f32[32,1,128]{2,1,0:T(1,128)} %copy-done.4, f32[2,512,512]{2,1,0:T(8,128)} %get-tuple-element.22.near_ref, bf16[1,512,512]{2,1,0:T(8,128)(2,1)} %copy-done.3, bf16[1,512,512]{2,1,0:T(8,128)(2,1)} %copy-done.2), custom_call_target="tpu_custom_call" | custom-call | tf_op jit(solution)/shard_map/factor_rows/pallas_call | solution.py:112
  (11 shorter events, 0.0 us)
Async XLA Ops:
  39.6 19.8 %all-to-all-start.2 = ((bf16[16,32,1024]{2,1,0:T(8,128)(2,1)}), bf16[16,32,1024]{2,1,0:T(8,128)(2,1)S(1)}, u32[]{:S(2)}, u32[]{:S(2)}) async-start(bf16[16,32,1024]{2,1,0:T(8,128)(2,1)} %bitcast.4), calls=%async_computation.2 | async-start | bytes 2097152 | tf_op jit(solution)/shard_map/all_to_all | solution.py:349
  59.4 1.0 copy-start.1
  60.4 55.9 %all-to-all-start = ((bf16[16,64,1024]{2,1,0:T(8,128)(2,1)}), bf16[16,64,1024]{2,1,0:T(8,128)(2,1)S(1)}, u32[]{:S(2)}, u32[]{:S(2)}) async-start(bf16[16,64,1024]{2,1,0:T(8,128)(2,1)} %bitcast.6), calls=%async_computation | async-start | bytes 4194304 | tf_op jit(solution)/shard_map/all_to_all | solution.py:349
  67.2 61.5 %collective-permute-start.3 = (bf16[1,512,512]{2,1,0:T(8,128)(2,1)}, bf16[1,512,512]{2,1,0:T(8,128)(2,1)S(1)}, u32[]{:S(2)}, u32[]{:S(2)}) collective-permute-start(bf16[1,512,512]{2,1,0:T(8,128)(2,1)} %get-tuple-element.24), channel_id=1, source_target_pairs={{0,16},{1,17},{2,18},{3,19},{4,20},{5,21},{6,22},{7,23},{8,24},{9,... | collective-permute-start | bytes 1572872 | tf_op jit(solution)/shard_map/ppermute | solution.py:360
  72.8 55.9 %collective-permute-start.2 = (bf16[1,512,512]{2,1,0:T(8,128)(2,1)}, bf16[1,512,512]{2,1,0:T(8,128)(2,1)S(1)}, u32[]{:S(2)}, u32[]{:S(2)}) collective-permute-start(bf16[1,512,512]{2,1,0:T(8,128)(2,1)} %get-tuple-element.23), channel_id=1, source_target_pairs={{0,16},{1,17},{2,18},{3,19},{4,20},{5,21},{6,22},{7,23},{8,24},{9,... | collective-permute-start | bytes 1572872 | tf_op jit(solution)/shard_map/ppermute | solution.py:360
  73.1 43.2 %collective-permute-start.1 = (f32[1,1,512]{2,1,0:T(1,128)}, f32[1,1,512]{2,1,0:T(1,128)S(1)}, u32[]{:S(2)}, u32[]{:S(2)}) collective-permute-start(f32[1,1,512]{2,1,0:T(1,128)} %get-tuple-element.20), channel_id=1, source_target_pairs={{0,16},{1,17},{2,18},{3,19},{4,20},{5,21},{6,22},{7,23},{8,24},{9,... | collective-permute-start | bytes 6152 | tf_op jit(solution)/shard_map/ppermute | solution.py:359
  75.7 40.6 %collective-permute-start = (f32[1,1,512]{2,1,0:T(1,128)}, f32[1,1,512]{2,1,0:T(1,128)S(1)}, u32[]{:S(2)}, u32[]{:S(2)}) collective-permute-start(f32[1,1,512]{2,1,0:T(1,128)} %get-tuple-element.18), channel_id=1, source_target_pairs={{0,16},{1,17},{2,18},{3,19},{4,20},{5,21},{6,22},{7,23},{8,24},{9,... | collective-permute-start | bytes 6152 | tf_op jit(solution)/shard_map/ppermute | solution.py:359
  116.3 0.6 copy-start.5
  116.3 0.6 copy-start.6
  116.9 1.3 copy-start
  122.6 13.1 %all-to-all-start.3 = ((f32[32,1,128]{2,1,0:T(1,128)}), f32[32,1,128]{2,1,0:T(1,128)S(1)}, u32[]{:S(2)}, u32[]{:S(2)}) async-start(f32[32,1,128]{2,1,0:T(1,128)} %get-tuple-element.21), calls=%async_computation.3 | async-start | bytes 32768 | tf_op jit(solution)/shard_map/all_to_all | solution.py:363
  128.7 7.0 %copy-start.2 = (bf16[1,512,512]{2,1,0:T(8,128)(2,1)}, bf16[1,512,512]{2,1,0:T(8,128)(2,1)S(1)}, u32[]{:S(2)}) copy-start(bf16[1,512,512]{2,1,0:T(8,128)(2,1)S(1)} %collective-permute-done.3.far_second_ref) | copy-start | bytes 1572868
  128.7 7.0 %copy-start.3 = (bf16[1,512,512]{2,1,0:T(8,128)(2,1)}, bf16[1,512,512]{2,1,0:T(8,128)(2,1)S(1)}, u32[]{:S(2)}) copy-start(bf16[1,512,512]{2,1,0:T(8,128)(2,1)S(1)} %collective-permute-done.2.far_first_ref) | copy-start | bytes 1572868
  135.7 0.6 copy-start.4

commit v4 on v3

--- a/solution.py
+++ b/solution.py
@@ -135,6 +135,11 @@
     return jnp.asarray(both.astype(np.float32)).astype(jnp.bfloat16)
 
 
+def paired(windows):
+    half = windows // 2
+    return half <= 16 and half & (half - 1) == 0
+
+
 def front_kernel(steps, capacity, quarter, vis_ref, noise_ref, part_ref, row_ref, pick_ref, bank_ref, parts_ref, first_ref, second_ref, spectra_ref, slot_ref, table_ref):
     step = pl.program_id(0)
     windows = pick_ref.shape[1]
@@ -184,6 +189,9 @@
         upper = lax.axis_index("win") * 2 >= lax.axis_size("win")
         shifted = jnp.where(names >= windows, names - windows, names + windows)
         ordered = jnp.where(upper, names, shifted)
+        if paired(windows):
+            mine = (lax.axis_index("win") * lax.axis_size("band") + lax.axis_index("band")) % (windows // 2)
+            ordered = jnp.where(ordered < windows, ordered, ordered ^ (2 * mine))
         split = ((ordered & 1) * (windows // 2) + ordered // 2) * capacity
         slot_ref[...] = jnp.where(ordered < windows, split, ordered * capacity) + order
 
@@ -215,6 +223,24 @@
         out_shape=jax.ShapeDtypeStruct((offset, spectral), jnp.bfloat16),
         in_specs=[pl.BlockSpec((1, count), lambda s: (0, 0)), pl.BlockSpec((count, spectral), lambda s: (0, 0))],
         out_specs=pl.BlockSpec((SLOTS, spectral), lambda s: (s, 0)),
+        name="near",
+    )(slots, spectra)
+
+
+def near_parts_kernel(offset, slot_ref, spectra_ref, *out_refs):
+    rows_each = out_refs[0].shape[0]
+    per_step = SLOTS // rows_each
+    for c in range(len(out_refs) // per_step):
+        rows = placed_rows(offset + c * SLOTS, slot_ref, spectra_ref)
+        for t in range(per_step):
+            out_refs[c * per_step + t][...] = rows[rows_each * t : rows_each * (t + 1)]
+
+
+def near_parts(slots, spectra, offset, half):
+    spectral = spectra.shape[1]
+    return pl.pallas_call(
+        functools.partial(near_parts_kernel, offset),
+        out_shape=[jax.ShapeDtypeStruct((offset // half, spectral), jnp.bfloat16)] * half,
         name="near",
     )(slots, spectra)
 
@@ -298,6 +324,49 @@
         trace_ref[...] = jnp.broadcast_to(lanes, trace_ref.shape)
 
 
+def power_kernel(rows_ref, power_ref):
+    sources, capacity, spectral = rows_ref.shape
+    size = spectral // 2
+    rows = rows_ref[...].reshape(sources * capacity, spectral).astype(jnp.float32)
+    total = jnp.sum(rows * rows, axis=0, keepdims=True)
+    power_ref[0] = total[:, :size] + total[:, size:]
+
+
+def far_power(incoming):
+    size = incoming.shape[2] // 2
+    return pl.pallas_call(
+        power_kernel, out_shape=jax.ShapeDtypeStruct((1, 1, size), jnp.float32), name="far_power"
+    )(incoming)
+
+
+def paired_moment_kernel(count, *refs):
+    parts, (first_ref, second_ref, packed_ref, trace_ref) = refs[:count], refs[count:]
+    capacity = parts[0].shape[0] // 2
+    powers = []
+    for g, far_ref in enumerate((first_ref, second_ref)):
+        rows = jnp.concatenate([part[capacity * g : capacity * (g + 1), :] for part in parts], axis=0)
+        packed, power = packed_moments(rows[None])
+        packed_ref[g] = packed
+        powers.append(power + far_ref[0])
+    both = 0.5 * powers[0] * powers[1]
+    lanes = both[:, :LANE]
+    for t in range(1, both.shape[1] // LANE):
+        lanes = lanes + both[:, LANE * t : LANE * (t + 1)]
+    trace_ref[...] = jnp.broadcast_to(lanes, trace_ref.shape)
+
+
+def paired_moments(parts, first, second, windows):
+    size = parts[0].shape[1] // 2
+    return pl.pallas_call(
+        functools.partial(paired_moment_kernel, len(parts)),
+        out_shape=[
+            jax.ShapeDtypeStruct((2, size, size), jnp.float32),
+            jax.ShapeDtypeStruct((windows, 1, LANE), jnp.float32),
+        ],
+        name="near_moments",
+    )(*parts, first, second)
+
+
 def far_moments(incoming):
     _, _, spectral = incoming.shape
     size = spectral // 2
@@ -351,15 +420,25 @@
         )
 
     *fars, spectra, slots = far_slots(vis, inv_noise, assign, taper_bank, taper_pick, windows, capacity)
-    near = near_slots(slots, spectra, windows * capacity)
+    if paired(windows):
+        parts = list(near_parts(slots, spectra, windows * capacity, half))
+    else:
+        near = near_slots(slots, spectra, windows * capacity)
     received, powers = [], []
-    for far in fars:
+    for g, far in enumerate(fars):
         far = gather_half(far)
         packed, power = far_moments(far)
+        if paired(windows) and g == 0:
+            power = far_power(far)
         powers.append(lax.ppermute(power, everywhere, mirror))
         received.append(lax.ppermute(packed, everywhere, mirror))
-    near = gather_half(near)
-    near, traces = near_moments(near, *powers, windows)
+    if paired(windows):
+        for k in range(1, half):
+            parts[k] = lax.ppermute(parts[k], everywhere, [(i, i ^ k) for i in range(windows)])
+        near, traces = paired_moments(parts, *powers, windows)
+    else:
+        near = gather_half(near)
+        near, traces = near_moments(near, *powers, windows)
     traces = lax.all_to_all(traces, everywhere, split_axis=0, concat_axis=0, tiled=True)
     return factor_rows(traces, near, *received)[None]
 

time: 155 us -> 165 us (1.065)
  blocking collectives: 22.6 us -> 33.2 us
  waiting for transfers between devices: 58.2 us -> 49.8 us
  starting transfers between devices: 19.3 us -> 25.5 us
  Pallas kernels: 50.9 us -> 53.1 us
    ppermute x0 -> x15, waiting for transfers between devices: none -> 45.9 us  [local(): lax.ppermute(parts[k], everywhere, [(i, i ^ k) for i in range(windows)])]
    ppermute x2, waiting for transfers between devices: 40.3 us -> 1.94 us  [local(): powers.append(lax.ppermute(power, everywhere, mirror))]
    ppermute x0 -> x15, starting transfers between devices: none -> 15.4 us  [local(): lax.ppermute(parts[k], everywhere, [(i, i ^ k) for i in range(windows)])]
    all_to_all x0 -> x1, blocking collectives: none -> 10.6 us  [local(): lax.all_to_all(traces, everywhere, split_axis=0, concat_axis=0, tiled=True)]
    all_to_all x2 -> x1, waiting for transfers between devices: 11 us -> 1.93 us  [gather_half(): lax.all_to_all(rows, everywhere, split_axis=0, concat_axis=0, axis_index_...]
    all_to_all x1 -> x0, waiting for transfers between devices: 6.95 us -> none  [local(): lax.all_to_all(traces, everywhere, split_axis=0, concat_axis=0, tiled=True)]
    all_to_all x1 -> x0, starting transfers between devices: 6.12 us -> none  [local(): lax.all_to_all(traces, everywhere, split_axis=0, concat_axis=0, tiled=True)]
    all_to_all x2 -> x1, starting transfers between devices: 7.37 us -> 3.65 us  [gather_half(): lax.all_to_all(rows, everywhere, split_axis=0, concat_axis=0, axis_index_...]
  transfers between devices with their start and end apart: 7 -> 20, of which waited for: 3 -> 11; matrix products, arithmetic and copies ran while one was open for 0% -> 0% of each run, Pallas kernels for 10% -> 11%
where the time goes in v4:
time: 165 us; the launch traced here: 164 us
  Pallas kernels  53.1 us (32%)
  waiting for transfers between devices  49.8 us (30%)
  blocking collectives  33.2 us (20%)
  starting transfers between devices  25.5 us (15%)
  local copies, waits for them, and re-layouts  2.43 us (1%)
    ppermute x15, waiting for transfers between devices, local(): lax.ppermute(parts[k], everywhere, [(i, i ^ k) for i in range(windows)])  45.9 us
    all_to_all x1, blocking collectives, gather_half(): lax.all_to_all(rows, everywhere, split_axis=0, concat_axis=0, axis_index_...  22.6 us
    pallas_call x1, Pallas kernels, factor_rows(): pl.pallas_call(factor_kernel, out_shape=jax.ShapeDtypeStruct((size, size)...  18.3 us
    pallas_call x1, Pallas kernels, far_slots(): pl.pallas_call(functools.partial(front_kernel, steps, capacity, quarter),...  17.2 us
    ppermute x15, starting transfers between devices, local(): lax.ppermute(parts[k], everywhere, [(i, i ^ k) for i in range(windows)])  15.4 us
    all_to_all x1, blocking collectives, local(): lax.all_to_all(traces, everywhere, split_axis=0, concat_axis=0, tiled=True)  10.6 us
    pallas_call x2, Pallas kernels, far_moments(): pl.pallas_call(far_kernel, out_shape=[jax.ShapeDtypeStruct((1, size, size...  6.07 us
    pallas_call x1, Pallas kernels, near_parts(): pl.pallas_call(functools.partial(near_parts_kernel, offset), out_shape=[j...  4.92 us
  transfers between devices with their start and end apart: 20, of which 11 were waited for; matrix products, arithmetic and copies ran while one was open for 0% of the time, Pallas kernels for 11%

profile of v4, /device:TPU:0, one launch (start us, length us, event | category | flops | bytes accessed | tf_op | source)
XLA Modules:
  0.0 164.3 jit_solution(14324096918305310930)
XLA Ops:
  0.0 17.2 %front.1 = (bf16[512,1024]{1,0:T(8,128)(2,1)}, bf16[512,1024]{1,0:T(8,128)(2,1)}, bf16[1024,1024]{1,0:T(8,128)(2,1)}, s32[1,1024]{1,0:T(1,128)}) custom-call(bf16[1024,2,1024]{2,1,0:T(2,128)(2,1)} %vis_ref.1, f32[1024,1024]{1,0:T(8,128)} %noise_ref.1, s32[1,1024]{1,0:T(1,128)} %bitcast.7, s32[1,1024]{1,0:T(1,128)} %bitcast.8, s32[1,32]{1,0:T(1,128)} %bitcast.9, ...), custom_call_target="tpu_custom_call" | custom-call | tf_op jit(solution)/shard_map/front/pallas_call | solution.py:259
  17.2 22.6 %all_to_all.15.rows_ref = bf16[16,32,1024]{2,1,0:T(8,128)(2,1)} all-to-all(bf16[16,32,1024]{2,1,0:T(8,128)(2,1)} %bitcast.6), channel_id=1, replica_groups={{0,1,2,3,4,5,6,7,8,9,10,11,12,13,14,15},{16,17,18,19,20,21,22,23,24,25,..., dimensions={0} | all-to-all | bytes 2097152 | tf_op jit(solution)/shard_map/all_to_all | solution.py:418
  39.7 3.7 %all-to-all-start.1 = ((bf16[16,32,1024]{2,1,0:T(8,128)(2,1)}), bf16[16,32,1024]{2,1,0:T(8,128)(2,1)S(1)}, u32[]{:S(2)}, u32[]{:S(2)}) async-start(bf16[16,32,1024]{2,1,0:T(8,128)(2,1)} %bitcast.5), calls=%async_computation.1 | async-start | bytes 2097152 | tf_op jit(solution)/shard_map/all_to_all | solution.py:418
  43.4 4.9 %near.1 = (bf16[64,1024]{1,0:T(8,128)(2,1)}, bf16[64,1024]{1,0:T(8,128)(2,1)}, bf16[64,1024]{1,0:T(8,128)(2,1)}, bf16[64,1024]{1,0:T(8,128)(2,1)}, bf16[64,1024]...) custom-call(s32[1,1024]{1,0:T(1,128)} %get-tuple-element.30.slot_ref, ...), custom_call_target="tpu_custom_call" | custom-call | tf_op jit(solution)/shard_map/near/pallas_call | solution.py:241
  50.2 1.7 %collective-permute-start.3 = (bf16[64,1024]{1,0:T(8,128)(2,1)}, bf16[64,1024]{1,0:T(8,128)(2,1)S(1)}, u32[]{:S(2)}, u32[]{:S(2)}) collective-permute-start(bf16[64,1024]{1,0:T(8,128)(2,1)} %get-tuple-element.36), channel_id=1, source_target_pairs={{0,4},{1,5},{2,6},{3,7},{4,0},{5,1},{6,2},{7,3},{8,12},{9,13},{10,... | collective-permute-start | bytes 393224 | tf_op jit(solution)/shard_map/ppermute | solution.py:437
  52.1 2.6 %collective-permute-start.5 = (bf16[64,1024]{1,0:T(8,128)(2,1)}, bf16[64,1024]{1,0:T(8,128)(2,1)S(1)}, u32[]{:S(2)}, u32[]{:S(2)}) collective-permute-start(bf16[64,1024]{1,0:T(8,128)(2,1)} %get-tuple-element.38), channel_id=1, source_target_pairs={{0,6},{1,7},{2,4},{3,5},{4,2},{5,3},{6,0},{7,1},{8,14},{9,15},{10,... | collective-permute-start | bytes 393224 | tf_op jit(solution)/shard_map/ppermute | solution.py:437
  54.7 3.0 %far_moments.3 = (bf16[1,512,512]{2,1,0:T(8,128)(2,1)}, f32[1,1,512]{2,1,0:T(1,128)}) custom-call(bf16[16,32,1024]{2,1,0:T(8,128)(2,1)} %all_to_all.15.rows_ref), custom_call_target="tpu_custom_call" | custom-call | tf_op jit(solution)/shard_map/far_moments/pallas_call | solution.py:373
  57.7 1.9 %all-to-all-done.1.rows_ref = bf16[16,32,1024]{2,1,0:T(8,128)(2,1)S(1)} async-done(((bf16[16,32,1024]{2,1,0:T(8,128)(2,1)}), bf16[16,32,1024]{2,1,0:T(8,128)(2,1)S(1)}, u32[]{:S(2)}, u32[]{:S(2)}) %all-to-all-start.1) | async-done | bytes 1048608 | tf_op jit(solution)/shard_map/all_to_all | solution.py:418
  60.6 3.0 %far_moments.2 = (bf16[1,512,512]{2,1,0:T(8,128)(2,1)}, f32[1,1,512]{2,1,0:T(1,128)}) custom-call(bf16[16,32,1024]{2,1,0:T(8,128)(2,1)} %copy-done), custom_call_target="tpu_custom_call" | custom-call | tf_op jit(solution)/shard_map/far_moments/pallas_call | solution.py:373
  63.6 2.6 %collective-permute-start.18 = (bf16[1,512,512]{2,1,0:T(8,128)(2,1)}, bf16[1,512,512]{2,1,0:T(8,128)(2,1)S(1)}, u32[]{:S(2)}, u32[]{:S(2)}) collective-permute-start(bf16[1,512,512]{2,1,0:T(8,128)(2,1)} %get-tuple-element.54), channel_id=1, source_target_pairs={{0,16},{1,17},{2,18},{3,19},{4,20},{5,21},{6,22},{7,23},{8,24},{9,... | collective-permute-start | bytes 1572872 | tf_op jit(solution)/shard_map/ppermute | solution.py:434
  69.4 3.2 %collective-permute-done.6.refs_7_ = bf16[64,1024]{1,0:T(8,128)(2,1)S(1)} collective-permute-done((bf16[64,1024]{1,0:T(8,128)(2,1)}, bf16[64,1024]{1,0:T(8,128)(2,1)S(1)}, u32[]{:S(2)}, u32[]{:S(2)}) %collective-permute-start.6) | collective-permute-done | bytes 131104 | tf_op jit(solution)/shard_map/ppermute | solution.py:437
  73.7 19.2 %collective-permute-done.7.refs_8_ = bf16[64,1024]{1,0:T(8,128)(2,1)S(1)} collective-permute-done((bf16[64,1024]{1,0:T(8,128)(2,1)}, bf16[64,1024]{1,0:T(8,128)(2,1)S(1)}, u32[]{:S(2)}, u32[]{:S(2)}) %collective-permute-start.7) | collective-permute-done | bytes 131104 | tf_op jit(solution)/shard_map/ppermute | solution.py:437
  93.4 2.4 %collective-permute-done.8.refs_9_ = bf16[64,1024]{1,0:T(8,128)(2,1)S(1)} collective-permute-done((bf16[64,1024]{1,0:T(8,128)(2,1)}, bf16[64,1024]{1,0:T(8,128)(2,1)S(1)}, u32[]{:S(2)}, u32[]{:S(2)}) %collective-permute-start.8) | collective-permute-done | bytes 131104 | tf_op jit(solution)/shard_map/ppermute | solution.py:437
  96.8 1.8 %collective-permute-done.9.refs_10_ = bf16[64,1024]{1,0:T(8,128)(2,1)S(1)} collective-permute-done((bf16[64,1024]{1,0:T(8,128)(2,1)}, bf16[64,1024]{1,0:T(8,128)(2,1)S(1)}, u32[]{:S(2)}, u32[]{:S(2)}) %collective-permute-start.9) | collective-permute-done | bytes 131104 | tf_op jit(solution)/shard_map/ppermute | solution.py:437
  98.6 1.9 %collective-permute-start.12 = (bf16[64,1024]{1,0:T(8,128)(2,1)}, bf16[64,1024]{1,0:T(8,128)(2,1)S(1)}, u32[]{:S(2)}, u32[]{:S(2)}) collective-permute-start(bf16[64,1024]{1,0:T(8,128)(2,1)} %get-tuple-element.45), channel_id=1, source_target_pairs={{0,13},{1,12},{2,15},{3,14},{4,9},{5,8},{6,11},{7,10},{8,5},{9,4},... | collective-permute-start | bytes 393224 | tf_op jit(solution)/shard_map/ppermute | solution.py:437
  100.4 14.1 %collective-permute-done.10.refs_11_ = bf16[64,1024]{1,0:T(8,128)(2,1)S(1)} collective-permute-done((bf16[64,1024]{1,0:T(8,128)(2,1)}, bf16[64,1024]{1,0:T(8,128)(2,1)S(1)}, u32[]{:S(2)}, u32[]{:S(2)}) %collective-permute-start.10) | collective-permute-done | bytes 131104 | tf_op jit(solution)/shard_map/ppermute | solution.py:437
  115.5 1.7 %collective-permute-done.11.refs_12_ = bf16[64,1024]{1,0:T(8,128)(2,1)S(1)} collective-permute-done((bf16[64,1024]{1,0:T(8,128)(2,1)}, bf16[64,1024]{1,0:T(8,128)(2,1)S(1)}, u32[]{:S(2)}, u32[]{:S(2)}) %collective-permute-start.11) | collective-permute-done | bytes 131104 | tf_op jit(solution)/shard_map/ppermute | solution.py:437
  117.9 1.9 %far_power.1 = f32[1,1,512]{2,1,0:T(1,128)} custom-call(bf16[16,32,1024]{2,1,0:T(8,128)(2,1)} %all_to_all.15.rows_ref), custom_call_target="tpu_custom_call" | custom-call | tf_op jit(solution)/shard_map/far_power/pallas_call | solution.py:337
  119.9 3.5 %collective-permute-start.16 = (f32[1,1,512]{2,1,0:T(1,128)}, f32[1,1,512]{2,1,0:T(1,128)S(1)}, u32[]{:S(2)}, u32[]{:S(2)}) collective-permute-start(f32[1,1,512]{2,1,0:T(1,128)} %get-tuple-element.50), channel_id=1, source_target_pairs={{0,16},{1,17},{2,18},{3,19},{4,20},{5,21},{6,22},{7,23},{8,24},{9,... | collective-permute-start | bytes 6152 | tf_op jit(solution)/shard_map/ppermute | solution.py:433
  124.3 2.7 %collective-permute-done.14.refs_15_ = bf16[64,1024]{1,0:T(8,128)(2,1)S(1)} collective-permute-done((bf16[64,1024]{1,0:T(8,128)(2,1)}, bf16[64,1024]{1,0:T(8,128)(2,1)S(1)}, u32[]{:S(2)}, u32[]{:S(2)}) %collective-permute-start.14) | collective-permute-done | bytes 131104 | tf_op jit(solution)/shard_map/ppermute | solution.py:437
  127.0 1.9 %collective-permute-done.15.refs_16_ = f32[1,1,512]{2,1,0:T(1,128)S(1)} collective-permute-done((f32[1,1,512]{2,1,0:T(1,128)}, f32[1,1,512]{2,1,0:T(1,128)S(1)}, u32[]{:S(2)}, u32[]{:S(2)}) %collective-permute-start.15) | collective-permute-done | bytes 2080 | tf_op jit(solution)/shard_map/ppermute | solution.py:433
  129.5 4.8 %near_moments.1 = (f32[2,512,512]{2,1,0:T(8,128)}, f32[32,1,128]{2,1,0:T(1,128)}) custom-call(bf16[64,1024]{1,0:T(8,128)(2,1)} %get-tuple-element.32.refs_0_, bf16[64,1024]{1,0:T(8,128)(2,1)} %copy-done.3, bf16[64,1024]{1,0:T(8,128)(2,1)} %copy-done.4, bf16[64,1024]{1,0:T(8,128)(2,1)} %copy-done.5, bf16[64,1024]{1,0:T(8,128)(2,1)} %copy-done.6, ...), custom_call_target="tpu_custom_call" | custom-call | tf_op jit(solution)/shard_map/near_moments/pallas_call | solution.py:360
  134.4 10.6 %all_to_all.16.trace_ref = f32[32,1,128]{2,1,0:T(1,128)} all-to-all(f32[32,1,128]{2,1,0:T(1,128)} %get-tuple-element.51), channel_id=1, replica_groups=mesh['win'=8,'band'=4] {'win','band'}, dimensions={0} | all-to-all | bytes 32768 | tf_op jit(solution)/shard_map/all_to_all | solution.py:442
  146.0 18.3 %factor_rows.1 = f32[512,512]{1,0:T(8,128)} custom-call(f32[32,1,128]{2,1,0:T(1,128)} %all_to_all.16.trace_ref, f32[2,512,512]{2,1,0:T(8,128)} %get-tuple-element.52.near_ref, bf16[1,512,512]{2,1,0:T(8,128)(2,1)} %copy-done.2, bf16[1,512,512]{2,1,0:T(8,128)(2,1)} %copy-done.1), custom_call_target="tpu_custom_call" | custom-call | tf_op jit(solution)/shard_map/factor_rows/pallas_call | solution.py:112
  (65 shorter events, 12.9 us)
Async XLA Ops:
  39.7 19.9 %all-to-all-start.1 = ((bf16[16,32,1024]{2,1,0:T(8,128)(2,1)}), bf16[16,32,1024]{2,1,0:T(8,128)(2,1)S(1)}, u32[]{:S(2)}, u32[]{:S(2)}) async-start(bf16[16,32,1024]{2,1,0:T(8,128)(2,1)} %bitcast.5), calls=%async_computation.1 | async-start | bytes 2097152 | tf_op jit(solution)/shard_map/all_to_all | solution.py:418
  48.3 3.8 %collective-permute-start = (bf16[64,1024]{1,0:T(8,128)(2,1)}, bf16[64,1024]{1,0:T(8,128)(2,1)S(1)}, u32[]{:S(2)}, u32[]{:S(2)}) collective-permute-start(bf16[64,1024]{1,0:T(8,128)(2,1)} %get-tuple-element.33), channel_id=1, source_target_pairs={{0,1},{1,0},{2,3},{3,2},{4,5},{5,4},{6,7},{7,6},{8,9},{9,8},{10,11... | collective-permute-start | bytes 393224 | tf_op jit(solution)/shard_map/ppermute | solution.py:437
  48.6 15.0 %collective-permute-start.1 = (bf16[64,1024]{1,0:T(8,128)(2,1)}, bf16[64,1024]{1,0:T(8,128)(2,1)S(1)}, u32[]{:S(2)}, u32[]{:S(2)}) collective-permute-start(bf16[64,1024]{1,0:T(8,128)(2,1)} %get-tuple-element.34), channel_id=1, source_target_pairs={{0,2},{1,3},{2,0},{3,1},{4,6},{5,7},{6,4},{7,5},{8,10},{9,11},{10,... | collective-permute-start | bytes 393224 | tf_op jit(solution)/shard_map/ppermute | solution.py:437
  50.2 16.0 %collective-permute-start.2 = (bf16[64,1024]{1,0:T(8,128)(2,1)}, bf16[64,1024]{1,0:T(8,128)(2,1)S(1)}, u32[]{:S(2)}, u32[]{:S(2)}) collective-permute-start(bf16[64,1024]{1,0:T(8,128)(2,1)} %get-tuple-element.35), channel_id=1, source_target_pairs={{0,3},{1,2},{2,1},{3,0},{4,7},{5,6},{6,5},{7,4},{8,11},{9,10},{10,... | collective-permute-start | bytes 393224 | tf_op jit(solution)/shard_map/ppermute | solution.py:437
  50.2 16.3 %collective-permute-start.3 = (bf16[64,1024]{1,0:T(8,128)(2,1)}, bf16[64,1024]{1,0:T(8,128)(2,1)S(1)}, u32[]{:S(2)}, u32[]{:S(2)}) collective-permute-start(bf16[64,1024]{1,0:T(8,128)(2,1)} %get-tuple-element.36), channel_id=1, source_target_pairs={{0,4},{1,5},{2,6},{3,7},{4,0},{5,1},{6,2},{7,3},{8,12},{9,13},{10,... | collective-permute-start | bytes 393224 | tf_op jit(solution)/shard_map/ppermute | solution.py:437
  52.0 15.5 %collective-permute-start.4 = (bf16[64,1024]{1,0:T(8,128)(2,1)}, bf16[64,1024]{1,0:T(8,128)(2,1)S(1)}, u32[]{:S(2)}, u32[]{:S(2)}) collective-permute-start(bf16[64,1024]{1,0:T(8,128)(2,1)} %get-tuple-element.37), channel_id=1, source_target_pairs={{0,5},{1,4},{2,7},{3,6},{4,1},{5,0},{6,3},{7,2},{8,13},{9,12},{10,... | collective-permute-start | bytes 393224 | tf_op jit(solution)/shard_map/ppermute | solution.py:437
  52.1 76.9 %copy-start.3 = (bf16[64,1024]{1,0:T(8,128)(2,1)}, bf16[64,1024]{1,0:T(8,128)(2,1)S(1)}, u32[]{:S(2)}) copy-start(bf16[64,1024]{1,0:T(8,128)(2,1)S(1)} %collective-permute-done.refs_1_) | copy-start | bytes 393220
  52.1 16.3 %collective-permute-start.5 = (bf16[64,1024]{1,0:T(8,128)(2,1)}, bf16[64,1024]{1,0:T(8,128)(2,1)S(1)}, u32[]{:S(2)}, u32[]{:S(2)}) collective-permute-start(bf16[64,1024]{1,0:T(8,128)(2,1)} %get-tuple-element.38), channel_id=1, source_target_pairs={{0,6},{1,7},{2,4},{3,5},{4,2},{5,3},{6,0},{7,1},{8,14},{9,15},{10,... | collective-permute-start | bytes 393224 | tf_op jit(solution)/shard_map/ppermute | solution.py:437
  63.6 65.3 %copy-start.4 = (bf16[64,1024]{1,0:T(8,128)(2,1)}, bf16[64,1024]{1,0:T(8,128)(2,1)S(1)}, u32[]{:S(2)}) copy-start(bf16[64,1024]{1,0:T(8,128)(2,1)S(1)} %collective-permute-done.1.refs_2_) | copy-start | bytes 393220
  63.6 81.4 %collective-permute-start.18 = (bf16[1,512,512]{2,1,0:T(8,128)(2,1)}, bf16[1,512,512]{2,1,0:T(8,128)(2,1)S(1)}, u32[]{:S(2)}, u32[]{:S(2)}) collective-permute-start(bf16[1,512,512]{2,1,0:T(8,128)(2,1)} %get-tuple-element.54), channel_id=1, source_target_pairs={{0,16},{1,17},{2,18},{3,19},{4,20},{5,21},{6,22},{7,23},{8,24},{9,... | collective-permute-start | bytes 1572872 | tf_op jit(solution)/shard_map/ppermute | solution.py:434
  66.3 62.7 %copy-start.5 = (bf16[64,1024]{1,0:T(8,128)(2,1)}, bf16[64,1024]{1,0:T(8,128)(2,1)S(1)}, u32[]{:S(2)}) copy-start(bf16[64,1024]{1,0:T(8,128)(2,1)S(1)} %collective-permute-done.2.refs_3_) | copy-start | bytes 393220
  66.3 78.7 %collective-permute-start.17 = (bf16[1,512,512]{2,1,0:T(8,128)(2,1)}, bf16[1,512,512]{2,1,0:T(8,128)(2,1)S(1)}, u32[]{:S(2)}, u32[]{:S(2)}) collective-permute-start(bf16[1,512,512]{2,1,0:T(8,128)(2,1)} %get-tuple-element.53), channel_id=1, source_target_pairs={{0,16},{1,17},{2,18},{3,19},{4,20},{5,21},{6,22},{7,23},{8,24},{9,... | collective-permute-start | bytes 1572872 | tf_op jit(solution)/shard_map/ppermute | solution.py:434
  66.6 62.4 %copy-start.6 = (bf16[64,1024]{1,0:T(8,128)(2,1)}, bf16[64,1024]{1,0:T(8,128)(2,1)S(1)}, u32[]{:S(2)}) copy-start(bf16[64,1024]{1,0:T(8,128)(2,1)S(1)} %collective-permute-done.3.refs_4_) | copy-start | bytes 393220
  66.6 6.0 %collective-permute-start.6 = (bf16[64,1024]{1,0:T(8,128)(2,1)}, bf16[64,1024]{1,0:T(8,128)(2,1)S(1)}, u32[]{:S(2)}, u32[]{:S(2)}) collective-permute-start(bf16[64,1024]{1,0:T(8,128)(2,1)} %get-tuple-element.39), channel_id=1, source_target_pairs={{0,7},{1,6},{2,5},{3,4},{4,3},{5,2},{6,1},{7,0},{8,15},{9,14},{10,... | collective-permute-start | bytes 393224 | tf_op jit(solution)/shard_map/ppermute | solution.py:437
  67.5 25.5 %collective-permute-start.7 = (bf16[64,1024]{1,0:T(8,128)(2,1)}, bf16[64,1024]{1,0:T(8,128)(2,1)S(1)}, u32[]{:S(2)}, u32[]{:S(2)}) collective-permute-start(bf16[64,1024]{1,0:T(8,128)(2,1)} %get-tuple-element.40), channel_id=1, source_target_pairs={{0,8},{1,9},{2,10},{3,11},{4,12},{5,13},{6,14},{7,15},{8,0},{9,1},... | collective-permute-start | bytes 393224 | tf_op jit(solution)/shard_map/ppermute | solution.py:437
  68.4 27.4 %collective-permute-start.8 = (bf16[64,1024]{1,0:T(8,128)(2,1)}, bf16[64,1024]{1,0:T(8,128)(2,1)S(1)}, u32[]{:S(2)}, u32[]{:S(2)}) collective-permute-start(bf16[64,1024]{1,0:T(8,128)(2,1)} %get-tuple-element.41), channel_id=1, source_target_pairs={{0,9},{1,8},{2,11},{3,10},{4,13},{5,12},{6,15},{7,14},{8,1},{9,0},... | collective-permute-start | bytes 393224 | tf_op jit(solution)/shard_map/ppermute | solution.py:437
  72.6 25.9 %collective-permute-start.9 = (bf16[64,1024]{1,0:T(8,128)(2,1)}, bf16[64,1024]{1,0:T(8,128)(2,1)S(1)}, u32[]{:S(2)}, u32[]{:S(2)}) collective-permute-start(bf16[64,1024]{1,0:T(8,128)(2,1)} %get-tuple-element.42), channel_id=1, source_target_pairs={{0,10},{1,11},{2,8},{3,9},{4,14},{5,15},{6,12},{7,13},{8,2},{9,3},... | collective-permute-start | bytes 393224 | tf_op jit(solution)/shard_map/ppermute | solution.py:437
  92.9 21.5 %collective-permute-start.10 = (bf16[64,1024]{1,0:T(8,128)(2,1)}, bf16[64,1024]{1,0:T(8,128)(2,1)S(1)}, u32[]{:S(2)}, u32[]{:S(2)}) collective-permute-start(bf16[64,1024]{1,0:T(8,128)(2,1)} %get-tuple-element.43), channel_id=1, source_target_pairs={{0,11},{1,10},{2,9},{3,8},{4,15},{5,14},{6,13},{7,12},{8,3},{9,2},... | collective-permute-start | bytes 393224 | tf_op jit(solution)/shard_map/ppermute | solution.py:437
  95.8 21.4 %collective-permute-start.11 = (bf16[64,1024]{1,0:T(8,128)(2,1)}, bf16[64,1024]{1,0:T(8,128)(2,1)S(1)}, u32[]{:S(2)}, u32[]{:S(2)}) collective-permute-start(bf16[64,1024]{1,0:T(8,128)(2,1)} %get-tuple-element.44), channel_id=1, source_target_pairs={{0,12},{1,13},{2,14},{3,15},{4,8},{5,9},{6,10},{7,11},{8,4},{9,5},... | collective-permute-start | bytes 393224 | tf_op jit(solution)/shard_map/ppermute | solution.py:437
  98.6 21.4 %collective-permute-start.12 = (bf16[64,1024]{1,0:T(8,128)(2,1)}, bf16[64,1024]{1,0:T(8,128)(2,1)S(1)}, u32[]{:S(2)}, u32[]{:S(2)}) collective-permute-start(bf16[64,1024]{1,0:T(8,128)(2,1)} %get-tuple-element.45), channel_id=1, source_target_pairs={{0,13},{1,12},{2,15},{3,14},{4,9},{5,8},{6,11},{7,10},{8,5},{9,4},... | collective-permute-start | bytes 393224 | tf_op jit(solution)/shard_map/ppermute | solution.py:437
  114.5 9.8 %collective-permute-start.13 = (bf16[64,1024]{1,0:T(8,128)(2,1)}, bf16[64,1024]{1,0:T(8,128)(2,1)S(1)}, u32[]{:S(2)}, u32[]{:S(2)}) collective-permute-start(bf16[64,1024]{1,0:T(8,128)(2,1)} %get-tuple-element.46), channel_id=1, source_target_pairs={{0,14},{1,15},{2,12},{3,13},{4,10},{5,11},{6,8},{7,9},{8,6},{9,7},... | collective-permute-start | bytes 393224 | tf_op jit(solution)/shard_map/ppermute | solution.py:437
  117.2 9.9 %collective-permute-start.14 = (bf16[64,1024]{1,0:T(8,128)(2,1)}, bf16[64,1024]{1,0:T(8,128)(2,1)S(1)}, u32[]{:S(2)}, u32[]{:S(2)}) collective-permute-start(bf16[64,1024]{1,0:T(8,128)(2,1)} %get-tuple-element.47), channel_id=1, source_target_pairs={{0,15},{1,14},{2,13},{3,12},{4,11},{5,10},{6,9},{7,8},{8,7},{9,6},... | collective-permute-start | bytes 393224 | tf_op jit(solution)/shard_map/ppermute | solution.py:437
  119.9 7.1 %collective-permute-start.16 = (f32[1,1,512]{2,1,0:T(1,128)}, f32[1,1,512]{2,1,0:T(1,128)S(1)}, u32[]{:S(2)}, u32[]{:S(2)}) collective-permute-start(f32[1,1,512]{2,1,0:T(1,128)} %get-tuple-element.50), channel_id=1, source_target_pairs={{0,16},{1,17},{2,18},{3,19},{4,20},{5,21},{6,22},{7,23},{8,24},{9,... | collective-permute-start | bytes 6152 | tf_op jit(solution)/shard_map/ppermute | solution.py:433
  124.3 4.7 %collective-permute-start.15 = (f32[1,1,512]{2,1,0:T(1,128)}, f32[1,1,512]{2,1,0:T(1,128)S(1)}, u32[]{:S(2)}, u32[]{:S(2)}) collective-permute-start(f32[1,1,512]{2,1,0:T(1,128)} %far_power.1), channel_id=1, source_target_pairs={{0,16},{1,17},{2,18},{3,19},{4,20},{5,21},{6,22},{7,23},{8,24},{9,... | collective-permute-start | bytes 6152 | tf_op jit(solution)/shard_map/ppermute | solution.py:433
  (16 other events, 326.4 us)
